TPU v7x, 128 devices: a whole 4x4x4 slice. The times are simulated.
128 devices in a mesh: dp: 16 (over x, z), expert: 8 (over y, core).
Axes of the slice: x: 4, y: 4, z: 4, core: 2. Of those that a mesh axis runs over, the one named last changes fastest.
Arguments:
- tokens: bfloat16 [16384, 2048], P(('dp', 'expert')), may hold values from -6 to 6
- out_grad: bfloat16 [16384, 2048], P(('dp', 'expert')), may hold values from -3 to 3
- z_weight: float32 [16384], P(('dp', 'expert')), may hold values from 0.1 to 1
- router_weight: bfloat16 [2048, 128], replicated, may hold values from -0.125 to 0.125
- expert_ids: int32 [16384, 4], P(('dp', 'expert')), may hold values from 0 to 127, as said below
- gate_up_weight: bfloat16 [8, 2048, 3072], P('expert'), may hold values from -0.125 to 0.125
- down_weight: bfloat16 [8, 1536, 2048], P('expert'), may hold values from -0.15625 to 0.15625
Outputs:
- token_grad: bfloat16 [16384, 2048], P(('dp', 'expert'))
- router_grad: float32 [2048, 128], replicated
- gate_up_grad: bfloat16 [8, 2048, 3072], P('expert', 'dp')
- down_grad: bfloat16 [8, 1536, 2048], P('expert', 'dp')
Inputs may be any that keep to these rules, and one draw needn't show every extreme that they name: `expert_ids`: each row names 4 different experts. Experts 0 to 7 are the ones in flight. The 128 rows of one device name any one expert in flight at most 64 times; in every data group some expert in flight is named exactly 64 times by the rows of each device of the group.
All inputs are finite; a program needn't handle non-finite values.
Results may differ from a plain program's by a relative error of at most 0.019.
Values may be sent and summed in bfloat16 or wider, within the bound.
A program may use at most 192 MiB of HBM per device.

v0:
```python
import jax
import jax.numpy as jnp
from jax import lax
from jax.sharding import PartitionSpec as P


def expert_rows(rows_in, rows_grad, w_gateup, w_down, acc_gateup, acc_down):
    hidden_units = w_down.shape[0]
    pre_act = jnp.dot(rows_in, w_gateup, preferred_element_type=jnp.float32)
    gate_pre = pre_act[:, :hidden_units]
    up_pre = pre_act[:, hidden_units:]
    activated = jax.nn.silu(gate_pre)
    hidden = (activated * up_pre).astype(jnp.bfloat16)
    expert_out = jnp.dot(hidden, w_down, preferred_element_type=jnp.float32).astype(jnp.bfloat16)
    hidden_grad = lax.dot_general(
        rows_grad, w_down, (((1,), (1,)), ((), ())), preferred_element_type=jnp.float32
    )
    acc_down = lax.dot_general(
        hidden, rows_grad, (((0,), (0,)), ((), ())), preferred_element_type=jnp.float32
    )
    sigmoid_gate = jax.nn.sigmoid(gate_pre)
    gate_grad = hidden_grad * up_pre * sigmoid_gate * (1.0 + gate_pre * (1.0 - sigmoid_gate))
    up_grad = hidden_grad * activated
    pre_grad = jnp.concatenate([gate_grad, up_grad], axis=1).astype(jnp.bfloat16)
    acc_gateup = lax.dot_general(
        rows_in, pre_grad, (((0,), (0,)), ((), ())), preferred_element_type=jnp.float32
    )
    input_grad = lax.dot_general(
        pre_grad, w_gateup, (((1,), (1,)), ((), ())), preferred_element_type=jnp.float32
    ).astype(jnp.bfloat16)
    return (acc_gateup, acc_down, expert_out, input_grad)


def split_pair(values):
    upper = values.astype(jnp.bfloat16)
    lower = (values - upper.astype(jnp.float32)).astype(jnp.bfloat16)
    return jnp.stack([upper, lower], axis=-1)


def join_pair(pair):
    return pair[..., 0].astype(jnp.float32) + pair[..., 1].astype(jnp.float32)


def per_device(tokens, out_grad, z_weight, router_weight, expert_ids, gate_up_weight, down_weight):
    tok_count, width = tokens.shape
    top_count = expert_ids.shape[1]
    routed = router_weight.shape[1]
    flight = lax.axis_size("expert")
    capacity = tok_count // 2
    w_gateup = gate_up_weight[0]
    w_down = down_weight[0]
    hidden_units = w_down.shape[0]
    logits = jnp.dot(tokens, router_weight, preferred_element_type=jnp.float32)
    choose = expert_ids[:, :, None] == jnp.arange(routed, dtype=jnp.int32)[None, None, :]
    selected = jnp.sum(jnp.where(choose, logits[:, None, :], 0.0), axis=2)
    sel_exp = jnp.exp(selected)
    probs = sel_exp / jnp.sum(sel_exp, axis=1, keepdims=True)
    log_total = jnp.log(jnp.sum(jnp.exp(logits), axis=1))
    flat_ids = expert_ids.reshape(-1)
    slot_count = tok_count * top_count
    member = (flat_ids[:, None] == jnp.arange(flight, dtype=jnp.int32)[None, :]).astype(jnp.int32)
    ranks = jnp.sum((jnp.cumsum(member, axis=0) - 1) * member, axis=1)
    in_flight = flat_ids < flight
    position = jnp.where(in_flight, flat_ids * capacity + ranks, flight * capacity)
    source_slot = (
        jnp.zeros((flight * capacity,), jnp.int32)
        .at[position]
        .set(jnp.arange(slot_count, dtype=jnp.int32), mode="drop")
    )
    filled = jnp.zeros((flight * capacity,), jnp.bool_).at[position].set(True, mode="drop")
    source_tok = source_slot // top_count
    send_in = jnp.where(filled[:, None], tokens[source_tok], 0)
    slot_prob = jnp.where(filled, probs.reshape(-1)[source_slot], 0.0)
    counts = jnp.sum(member, axis=0)
    count_msg = jnp.stack([counts // 128, counts % 128], axis=1).astype(jnp.bfloat16)
    send_raw = jnp.where(filled[:, None], out_grad[source_tok], 0)
    prob_pair = split_pair(slot_prob)
    recv_in, recv_raw, recv_prob, recv_counts = (
        lax.all_to_all(
            send_in.reshape(flight, capacity, width),
            "expert",
            split_axis=0,
            concat_axis=0,
            tiled=True,
        ),
        lax.all_to_all(
            send_raw.reshape(flight, capacity, width),
            "expert",
            split_axis=0,
            concat_axis=0,
            tiled=True,
        ),
        lax.all_to_all(
            prob_pair.reshape(flight, capacity, 2),
            "expert",
            split_axis=0,
            concat_axis=0,
            tiled=True,
        ),
        lax.all_to_all(count_msg, "expert", split_axis=0, concat_axis=0, tiled=True),
    )
    sources = recv_in.shape[0]
    total_rows = sources * capacity
    flat_in = recv_in.reshape(total_rows, width)
    flat_raw = recv_raw.reshape(total_rows, width)
    row_prob = join_pair(recv_prob.reshape(total_rows, 2))
    flat_grad = (row_prob[:, None] * flat_raw.astype(jnp.float32)).astype(jnp.bfloat16)
    acc_gateup, acc_down, produced, back_rows = expert_rows(
        flat_in,
        flat_grad,
        w_gateup,
        w_down,
        jnp.zeros((width, 2 * hidden_units), jnp.float32),
        jnp.zeros((hidden_units, width), jnp.float32),
    )
    slot_at = jnp.where(in_flight, position, 0)
    row_score = jnp.sum(flat_raw.astype(jnp.float32) * produced.astype(jnp.float32), axis=1)
    score_pair = split_pair(row_score)
    home_dx, home_pair = (
        lax.all_to_all(
            back_rows.reshape(sources, capacity, width),
            "expert",
            split_axis=0,
            concat_axis=0,
            tiled=True,
        ),
        lax.all_to_all(
            score_pair.reshape(sources, capacity, 2),
            "expert",
            split_axis=0,
            concat_axis=0,
            tiled=True,
        ),
    )
    flat_dx = home_dx.reshape(flight * capacity, width)
    flat_score = join_pair(home_pair.reshape(flight * capacity, 2))
    scores = jnp.where(in_flight, flat_score[slot_at], 0.0).reshape(tok_count, top_count)
    slot_dx = jnp.where(in_flight[:, None], flat_dx[slot_at], 0).reshape(
        tok_count, top_count, width
    )
    mean_score = jnp.sum(probs * scores, axis=1, keepdims=True)
    sel_grad = probs * (scores - mean_score)
    z_grad = 2.0 * z_weight[:, None] * log_total[:, None] * jnp.exp(logits - log_total[:, None])
    logit_grad = (z_grad + jnp.sum(jnp.where(choose, sel_grad[:, :, None], 0.0), axis=1)).astype(
        jnp.bfloat16
    )
    token_grad = (
        jnp.sum(slot_dx.astype(jnp.float32), axis=1)
        + lax.dot_general(
            logit_grad, router_weight, (((1,), (1,)), ((), ())), preferred_element_type=jnp.float32
        )
    ).astype(jnp.bfloat16)
    router_part = lax.dot_general(
        tokens, logit_grad, (((0,), (0,)), ((), ())), preferred_element_type=jnp.float32
    )
    router_grad = lax.psum(router_part, ("dp", "expert"))
    part_gateup = acc_gateup.astype(jnp.bfloat16)
    part_down = acc_down.astype(jnp.bfloat16)
    gate_up_grad, down_grad = (
        lax.psum_scatter(part_gateup[None], "dp", scatter_dimension=1, tiled=True).astype(
            jnp.float32
        ),
        lax.psum_scatter(part_down[None], "dp", scatter_dimension=1, tiled=True).astype(
            jnp.float32
        ),
    )
    return (
        token_grad,
        router_grad,
        gate_up_grad.astype(jnp.bfloat16),
        down_grad.astype(jnp.bfloat16),
    )


def solution(mesh):
    return jax.shard_map(
        per_device,
        mesh=mesh,
        in_specs=(
            P(("dp", "expert"), None),
            P(("dp", "expert"), None),
            P(("dp", "expert")),
            P(),
            P(("dp", "expert"), None),
            P("expert", None, None),
            P("expert", None, None),
        ),
        out_specs=(
            P(("dp", "expert"), None),
            P(),
            P("expert", "dp", None),
            P("expert", "dp", None),
        ),
        check_vma=False,
    )
```

profile of v0, /device:TPU:0, one launch (start us, length us, event | category | flops | bytes accessed | tf_op | source)
XLA Modules:
  0.0 320.7 jit_solution(609169090827551552)
XLA Ops:
  20.0 3.3 %gather_fusion.1 = bf16[512,2048]{1,0:T(8,128)(2,1)} fusion(bf16[128,2048]{1,0:T(8,128)(2,1)S(1)} %copy-done.2, s32[1024]{0:T(1024)S(1)} %get-tuple-element.42), kind=kCustom, calls=%fused_computation.1 | custom fusion | bytes 4196352 | tf_op jit(solution)/shard_map/gather | solution.py:76
  23.3 4.0 %broadcast_select_fusion = (bf16[8,64,2048]{2,1,0:T(8,128)(2,1)}, bf16[8,64,2048]{2,1,0:T(8,128)(2,1)}) fusion(bf16[8,64,2048]{2,1,0:T(8,128)(2,1)S(1)} %bitcast.69, pred[8,64]{1,0:T(8,128)(4,1)S(1)} %broadcast_in_dim.108, bf16[8,64,2048]{2,1,0:T(8,128)(2,1)} %bitcast.70), kind=kLoop, calls=%fused_computation.36 | loop fusion | flops 2097152 | bytes 8389120 | tf_op jit(solution)/shard_map/jit(_where)/select_n | solution.py:72
  27.4 4.7 %all-to-all-start.2 = ((bf16[8,64,2048]{2,1,0:T(8,128)(2,1)}), bf16[8,64,2048]{2,1,0:T(8,128)(2,1)S(1)}, u32[]{:S(2)}, u32[]{:S(2)}) async-start(bf16[8,64,2048]{2,1,0:T(8,128)(2,1)} %get-tuple-element.36), calls=%async_computation.2 | async-start | bytes 4194304 | tf_op jit(solution)/shard_map/all_to_all | solution.py:79
  32.9 26.4 %all-to-all-done.2 = bf16[8,64,2048]{2,1,0:T(8,128)(2,1)S(1)} async-done(((bf16[8,64,2048]{2,1,0:T(8,128)(2,1)}), bf16[8,64,2048]{2,1,0:T(8,128)(2,1)S(1)}, u32[]{:S(2)}, u32[]{:S(2)}) %all-to-all-start.2) | async-done | bytes 2097184 | tf_op jit(solution)/shard_map/all_to_all | solution.py:79
  60.6 3.8 %all-to-all-start.1 = ((bf16[8,64,2048]{2,1,0:T(8,128)(2,1)}), bf16[8,64,2048]{2,1,0:T(8,128)(2,1)S(1)}, u32[]{:S(2)}, u32[]{:S(2)}) async-start(bf16[8,64,2048]{2,1,0:T(8,128)(2,1)} %get-tuple-element.37), calls=%async_computation.1 | async-start | bytes 4194304 | tf_op jit(solution)/shard_map/all_to_all | solution.py:86
  64.4 9.9 %fusion.2 = f32[512,3072]{1,0:T(8,128)S(1)} fusion(bf16[512,2048]{1,0:T(8,128)(2,1)} %bitcast.72, bf16[1,2048,3072]{2,1,0:T(8,128)(2,1)} %param.12), kind=kOutput, calls=%fused_computation.9 | convolution fusion | flops 6442450944 | bytes 20971520 | tf_op jit(solution)/shard_map/dot_general | solution.py:9
  79.1 12.2 %all-to-all-done.1 = bf16[8,64,2048]{2,1,0:T(8,128)(2,1)S(1)} async-done(((bf16[8,64,2048]{2,1,0:T(8,128)(2,1)}), bf16[8,64,2048]{2,1,0:T(8,128)(2,1)S(1)}, u32[]{:S(2)}, u32[]{:S(2)}) %all-to-all-start.1) | async-done | bytes 2097184 | tf_op jit(solution)/shard_map/all_to_all | solution.py:86
  91.3 6.8 %fusion.10 = f32[512]{0:T(512)S(1)} fusion(bf16[8,64,2048]{2,1,0:T(8,128)(2,1)S(1)} %all-to-all-done.1, bf16[512,1536]{1,0:T(8,128)(2,1)} %multiply_convert_fusion, bf16[1,1536,2048]{2,1,0:T(8,128)(2,1)} %param.13), kind=kOutput, calls=%fused_computation.22 | convolution fusion | flops 3226467840 | bytes 9963520 | tf_op jit(solution)/shard_map/dot_general | solution.py:14
  98.8 3.3 %all-to-all-start.4 = ((bf16[8,64,2]{1,2,0:T(2,128)(2,1)}), bf16[8,64,2]{1,2,0:T(2,128)(2,1)S(1)}, u32[]{:S(2)}, u32[]{:S(2)}) async-start(bf16[8,64,2]{1,2,0:T(2,128)(2,1)} %copy.51), calls=%async_computation.4 | async-start | bytes 8192 | tf_op jit(solution)/shard_map/all_to_all | solution.py:127
  102.1 5.1 %all-to-all-done.4 = bf16[8,64,2]{1,2,0:T(2,128)(2,1)S(1)} async-done(((bf16[8,64,2]{1,2,0:T(2,128)(2,1)}), bf16[8,64,2]{1,2,0:T(2,128)(2,1)S(1)}, u32[]{:S(2)}, u32[]{:S(2)}) %all-to-all-start.4) | async-done | bytes 2080 | tf_op jit(solution)/shard_map/all_to_all | solution.py:127
  107.3 3.5 %gather_fusion.4 = f32[512]{0:T(512)S(1)} fusion(f32[512]{0:T(512)S(1)} %bitcast.67, s32[1024]{0:T(1024)S(1)} %pad_clamp_fusion), kind=kCustom, calls=%fused_computation.4 | custom fusion | bytes 6144 | tf_op jit(solution)/shard_map/gather | solution.py:137
  111.3 3.5 %gather_fusion = f32[512]{0:T(512)S(1)} fusion(f32[512]{0:T(512)S(1)} %div.31, s32[1024]{0:T(1024)S(1)} %get-tuple-element.43), kind=kCustom, calls=%fused_computation | custom fusion | bytes 6144 | tf_op jit(solution)/shard_map/gather | solution.py:73
  115.6 3.3 %all-to-all-start = ((bf16[8,64,2]{1,2,0:T(2,128)(2,1)}), bf16[8,64,2]{1,2,0:T(2,128)(2,1)S(1)}, u32[]{:S(2)}, u32[]{:S(2)}) async-start(bf16[8,64,2]{1,2,0:T(2,128)(2,1)} %copy.49), calls=%async_computation | async-start | bytes 8192 | tf_op jit(solution)/shard_map/all_to_all | solution.py:93
  120.6 3.4 %all-to-all-done = bf16[8,64,2]{1,2,0:T(2,128)(2,1)S(1)} async-done(((bf16[8,64,2]{1,2,0:T(2,128)(2,1)}), bf16[8,64,2]{1,2,0:T(2,128)(2,1)S(1)}, u32[]{:S(2)}, u32[]{:S(2)}) %all-to-all-start) | async-done | bytes 2080 | tf_op jit(solution)/shard_map/all_to_all | solution.py:93
  126.1 5.4 %fusion.4 = bf16[1,1536,2048]{2,1,0:T(8,128)(2,1)} fusion(bf16[512,1536]{1,0:T(8,128)(2,1)S(1)} %copy-done.7, bf16[512,2048]{1,0:T(8,128)(2,1)S(1)} %fusion.11), kind=kOutput, calls=%fused_computation.13 | convolution fusion | flops 3224371200 | bytes 9961472 | tf_op jit(solution)/shard_map/dot_general | solution.py:18
  132.3 8.4 %multiply_convert_fusion.2 = (bf16[512,1536]{1,0:T(8,128)(2,1)S(1)}, bf16[512,1536]{1,0:T(8,128)(2,1)S(1)}) fusion(f32[512,3072]{1,0:T(8,128)} %copy-done.3, bf16[512,2048]{1,0:T(8,128)(2,1)S(1)} %bitcast.71, bf16[1,1536,2048]{2,1,0:T(8,128)(2,1)} %param.13), kind=kOutput, calls=%fused_computation.28 | convolution fusion | flops 3231449088 | bytes 17825792 | tf_op jit(solution)/shard_map/dot_general | solution.py:15
  141.9 9.9 %convert_bitcast_fusion = bf16[1,2048,3072]{2,1,0:T(8,128)(2,1)} fusion(bf16[512,2048]{1,0:T(8,128)(2,1)S(1)} %bitcast.73, bf16[512,1536]{1,0:T(8,128)(2,1)S(1)} %get-tuple-element.31, bf16[512,1536]{1,0:T(8,128)(2,1)S(1)} %get-tuple-element.30), kind=kOutput, calls=%fused_computation.11 | convolution fusion | flops 6455033856 | bytes 17825792 | tf_op jit(solution)/shard_map/dot_general | solution.py:25
  151.8 11.3 %fusion.13 = bf16[512,2048]{1,0:T(8,128)(2,1)} fusion(bf16[1,2048,3072]{2,1,0:T(8,128)(2,1)} %param.12, bf16[512,1536]{1,0:T(8,128)(2,1)} %copy-done.10, bf16[512,1536]{1,0:T(8,128)(2,1)S(1)} %get-tuple-element.30), kind=kOutput, calls=%fused_computation.31 | convolution fusion | flops 6449790976 | bytes 17825792 | tf_op jit(solution)/shard_map/dot_general | solution.py:28
  163.1 3.9 %all-to-all-start.3 = ((bf16[8,64,2048]{2,1,0:T(8,128)(2,1)}), bf16[8,64,2048]{2,1,0:T(8,128)(2,1)S(1)}, u32[]{:S(2)}, u32[]{:S(2)}) async-start(bf16[8,64,2048]{2,1,0:T(8,128)(2,1)} %bitcast.74), calls=%async_computation.3 | async-start | bytes 4194304 | tf_op jit(solution)/shard_map/all_to_all | solution.py:120
  166.9 118.8 %all-reduce.2.cloned.1.call-done = f32[2048,128]{0,1:T(8,128)} async-done(((f32[2048,128]{0,1:T(8,128)}), f32[2048,128]{0,1:T(8,128)}) %all-reduce.2.cloned.1.call-update) | async-done | bytes 1048592 | tf_op jit(solution)/shard_map/psum | solution.py:156
  288.3 3.3 %gather_fusion.3 = bf16[512,2048]{1,0:T(8,128)(2,1)} fusion(bf16[512,2048]{1,0:T(8,128)(2,1)S(1)} %bitcast.68, s32[1024]{0:T(1024)S(1)} %pad_clamp_fusion), kind=kCustom, calls=%fused_computation.3 | custom fusion | bytes 4196352 | tf_op jit(solution)/shard_map/gather | solution.py:138
  291.6 2.8 gather.29
  294.4 3.9 %convert_reduce_fusion = f32[128,2048]{1,0:T(8,128)S(1)} fusion(bf16[128,4,2048]{2,1,0:T(4,128)(2,1)S(1)} %gather.29, pred[128,4]{1,0:T(8,128)(4,1)S(1)} %copy.42), kind=kLoop, calls=%fused_computation.24 | loop fusion | flops 2883584 | bytes 3146240 | tf_op jit(solution)/shard_map/reduce_sum | solution.py:148
  299.4 13.9 %reduce-scatter.3.cloned.1.call-done = bf16[1,128,3072]{2,1,0:T(8,128)(2,1)} async-done(((bf16[1,2048,3072]{2,1,0:T(8,128)(2,1)}), bf16[1,128,3072]{2,1,0:T(8,128)(2,1)}) %reduce-scatter.3.cloned.1.call-update) | async-done | bytes 786448 | tf_op jit(solution)/shard_map/reduce_scatter | solution.py:160
  (93 shorter events, 30.1 us)
Async XLA Ops:
  8.0 9.5 %copy-start = (bf16[128,2048]{1,0:T(8,128)(2,1)S(1)}, bf16[128,2048]{1,0:T(8,128)(2,1)}, u32[]{:S(2)}) copy-start(bf16[128,2048]{1,0:T(8,128)(2,1)} %param.7) | copy-start | bytes 1572868
  17.5 2.5 copy-start.2
  27.4 4.7 %copy-start.6 = (bf16[2048,128]{1,0:T(8,128)(2,1)S(1)}, bf16[2048,128]{1,0:T(8,128)(2,1)}, u32[]{:S(2)}) copy-start(bf16[2048,128]{1,0:T(8,128)(2,1)} %param.10) | copy-start | bytes 1572868
  27.4 5.2 %copy-start.8 = (s32[128,4]{0,1:T(4,128)S(1)}, s32[128,4]{0,1:T(4,128)}, u32[]{:S(2)}) copy-start(s32[128,4]{0,1:T(4,128)} %param.11) | copy-start | bytes 6148
  27.4 5.5 %copy-start.9 = (f32[128]{0:T(128)S(1)}, f32[128]{0:T(128)}, u32[]{:S(2)}) copy-start(f32[128]{0:T(128)} %param.9) | copy-start | bytes 1540
  27.4 31.9 %all-to-all-start.2 = ((bf16[8,64,2048]{2,1,0:T(8,128)(2,1)}), bf16[8,64,2048]{2,1,0:T(8,128)(2,1)S(1)}, u32[]{:S(2)}, u32[]{:S(2)}) async-start(bf16[8,64,2048]{2,1,0:T(8,128)(2,1)} %get-tuple-element.36), calls=%async_computation.2 | async-start | bytes 4194304 | tf_op jit(solution)/shard_map/all_to_all | solution.py:79
  59.3 1.3 copy-start.4
  60.6 30.7 %all-to-all-start.1 = ((bf16[8,64,2048]{2,1,0:T(8,128)(2,1)}), bf16[8,64,2048]{2,1,0:T(8,128)(2,1)S(1)}, u32[]{:S(2)}, u32[]{:S(2)}) async-start(bf16[8,64,2048]{2,1,0:T(8,128)(2,1)} %get-tuple-element.37), calls=%async_computation.1 | async-start | bytes 4194304 | tf_op jit(solution)/shard_map/all_to_all | solution.py:86
  74.4 2.7 copy-start.3
  98.8 8.5 %all-to-all-start.4 = ((bf16[8,64,2]{1,2,0:T(2,128)(2,1)}), bf16[8,64,2]{1,2,0:T(2,128)(2,1)S(1)}, u32[]{:S(2)}, u32[]{:S(2)}) async-start(bf16[8,64,2]{1,2,0:T(2,128)(2,1)} %copy.51), calls=%async_computation.4 | async-start | bytes 8192 | tf_op jit(solution)/shard_map/all_to_all | solution.py:127
  115.6 8.5 %all-to-all-start = ((bf16[8,64,2]{1,2,0:T(2,128)(2,1)}), bf16[8,64,2]{1,2,0:T(2,128)(2,1)S(1)}, u32[]{:S(2)}, u32[]{:S(2)}) async-start(bf16[8,64,2]{1,2,0:T(2,128)(2,1)} %copy.49), calls=%async_computation | async-start | bytes 8192 | tf_op jit(solution)/shard_map/all_to_all | solution.py:93
  118.9 166.8 %all-reduce.2.cloned.1.call-start = ((), (), s32[]{:S(2)}) async-start(), calls=%async_computation.7 | async-start | bytes 2097152 | tf_op jit(solution)/shard_map/psum | solution.py:156
  120.6 178.8 %reduce-scatter.5.cloned.1.call-start = ((), (), s32[]{:S(2)}) async-start(), calls=%async_computation.9 | async-start | bytes 6684672 | tf_op jit(solution)/shard_map/reduce_scatter | solution.py:163
  124.7 1.4 copy-start.7
  131.5 181.8 %reduce-scatter.3.cloned.1.call-start = ((), (), s32[]{:S(2)}) async-start(), calls=%async_computation.8 | async-start | bytes 13369344 | tf_op jit(solution)/shard_map/reduce_scatter | solution.py:160
  132.2 9.6 %copy-start.5 = (bf16[8,64,2048]{2,1,0:T(8,128)(2,1)S(1)}, bf16[8,64,2048]{2,1,0:T(8,128)(2,1)}, u32[]{:S(2)}) copy-start(bf16[8,64,2048]{2,1,0:T(8,128)(2,1)} %copy-done.4) | copy-start | bytes 6291460
  140.7 1.2 copy-start.10
  163.1 125.2 %all-to-all-start.3 = ((bf16[8,64,2048]{2,1,0:T(8,128)(2,1)}), bf16[8,64,2048]{2,1,0:T(8,128)(2,1)S(1)}, u32[]{:S(2)}, u32[]{:S(2)}) async-start(bf16[8,64,2048]{2,1,0:T(8,128)(2,1)} %bitcast.74), calls=%async_computation.3 | async-start | bytes 4194304 | tf_op jit(solution)/shard_map/all_to_all | solution.py:120
  291.6 21.7 %copy-start.1 = (bf16[128,2048]{1,0:T(8,128)(2,1)S(1)}, bf16[128,2048]{1,0:T(8,128)(2,1)}, u32[]{:S(2)}) copy-start(bf16[128,2048]{1,0:T(8,128)(2,1)} %param.7) | copy-start | bytes 1572868
Sparse Core Ops, SparseCore 0:
  125.1 160.5 all-reduce.1
Sparse Core Ops, SparseCore 1:
  131.6 82.6 reduce-scatter.4
  218.1 95.1 reduce-scatter.2
where the time goes:
time: 321 us
  waiting for transfers between devices  180 us (56%)
  matrix products  54.4 us (17%)
  local copies, waits for them, and re-layouts  36.3 us (11%)
  starting transfers between devices  19.3 us (6%)
  between operations  15.8 us (5%)
  other arithmetic  15 us (5%)
    psum x1, waiting for transfers between devices, per_device(): router_grad = lax.psum(router_part, ('dp', 'expert'))  119 us
    all_to_all x1, waiting for transfers between devices, per_device(): lax.all_to_all(send_in.reshape(flight, capacity, width), 'expert', split_...  26.4 us
    reduce_scatter x1, waiting for transfers between devices, per_device(): lax.psum_scatter(part_gateup[None], 'dp', scatter_dimension=1, tiled=True)  13.9 us
    all_to_all x1, waiting for transfers between devices, per_device(): lax.all_to_all(send_raw.reshape(flight, capacity, width), 'expert', split...  12.2 us
    dot_general x1, matrix products, expert_rows(): lax.dot_general(pre_grad, w_gateup, (((1,), (1,)), ((), ())), preferred_e...  11.3 us
    dot_general x1, matrix products, expert_rows(): pre_act = jnp.dot(rows_in, w_gateup, preferred_element_type=jnp.float32)  9.94 us
    dot_general x1, matrix products, expert_rows(): lax.dot_general(rows_in, pre_grad, (((0,), (0,)), ((), ())), preferred_el...  9.88 us
    unnamed x24, local copies, waits for them, and re-layouts  8.78 us
  transfers between devices with their start and end apart: 8, of which 6 were waited for; matrix products, arithmetic and copies ran while one was open for 20% of the time, Pallas kernels for 0%

commit v1 on v0

v1 whole, which is shorter than its diff:
```python
import functools

import jax
import jax.numpy as jnp
from jax import lax
from jax.experimental import pallas as pl
from jax.experimental.pallas import tpu as pltpu
from jax.sharding import PartitionSpec as P

BF = jnp.bfloat16
F32 = jnp.float32
MESH = pl.DeviceIdType.MESH

TOK = 128
CAP = 64
D = 2048
FF = 1536
SRC = 8
ROWS = SRC * CAP
ROUTED = 128
ND = D // 256
NG = 2 * FF // 256
NC = ND + NG
LAG1, LAG2, LAG3, LAG4 = 1, 3, 4, 6
DEP = 6
RING = 8
INV = (0, 1, 4, 5, 2, 3, 6, 7)


def nt(a, b):
    return lax.dot_general(a, b, (((1,), (1,)), ((), ())), preferred_element_type=F32)


def tn(a, b):
    return lax.dot_general(a, b, (((0,), (0,)), ((), ())), preferred_element_type=F32)


def nn(a, b):
    return jnp.dot(a, b, preferred_element_type=F32)


def kernel(
    tokens_hbm, grad_hbm, z_ref, rw_ref, ids_ref, gu_hbm, dn_hbm,
    tg_out, lg_out, gug_out, dng_out,
    xa, oa, meta, prob, logit, xr, xt, dy, hid, hidt, pg, gu, dn,
    part, r1, r2, rg, rb, sel, psum, psend, precv,
    lsem, ag_s, ag_r, mt_s, mt_r, ps_s, ps_r, rt_s, rt_r, s1, q1, s2, q2,
):
    dp = lax.axis_index("dp")
    ex = lax.axis_index("expert")
    px, pz = dp // 4, dp % 4
    py, pc = ex // 2, ex % 2
    xp, xm = ((px + 1) % 4) * 4 + pz, ((px + 3) % 4) * 4 + pz
    zp, zm = px * 4 + (pz + 1) % 4, px * 4 + (pz + 3) % 4
    yp, ym, yo = (py + 1) % 4, (py + 3) % 4, (py + 2) % 4
    oc = 1 - pc
    place = (ex, py * 2 + oc, ym * 2 + pc, ym * 2 + oc, yp * 2 + pc, yp * 2 + oc, yo * 2 + pc, yo * 2 + oc)

    cp_tok = pltpu.make_async_copy(tokens_hbm, xa.at[0], lsem.at[0])
    cp_grad = pltpu.make_async_copy(grad_hbm, oa.at[0], lsem.at[1])
    cp_gu = pltpu.make_async_copy(gu_hbm, gu, lsem.at[2])
    cp_dn = pltpu.make_async_copy(dn_hbm, dn, lsem.at[3])
    cp_tok.start()
    cp_grad.start()
    cp_gu.start()
    cp_dn.start()

    barrier = pltpu.get_barrier_semaphore()
    for to in (xp, xm, zp, zm):
        pl.semaphore_signal(barrier, inc=1, device_id=(to, ex), device_id_type=MESH)
    for q in range(1, SRC):
        pl.semaphore_signal(barrier, inc=1, device_id=(dp, place[q]), device_id_type=MESH)
    pl.semaphore_wait(barrier, 4 + SRC - 1)

    def ag(arr, buf, src_q, half, to_q, dst_q, k):
        rows = pl.ds(half * CAP, CAP)
        return pltpu.make_async_remote_copy(
            src_ref=buf.at[src_q, rows], dst_ref=buf.at[dst_q, rows],
            send_sem=ag_s.at[arr, k], recv_sem=ag_r.at[arr, dst_q, half],
            device_id=(dp, place[to_q]), device_id_type=MESH,
        )

    def ag_wait(arr, buf, q, half):
        rows = pl.ds(half * CAP, CAP)
        pltpu.make_async_remote_copy(
            src_ref=buf.at[q, rows], dst_ref=buf.at[q, rows],
            send_sem=ag_s.at[arr, 0], recv_sem=ag_r.at[arr, q, half],
            device_id=(dp, place[1]), device_id_type=MESH,
        ).wait_recv()

    def ag_own(arr, buf):
        out = [
            ag(arr, buf, 0, 0, 4, 2, 0), ag(arr, buf, 0, 1, 2, 4, 1),
            ag(arr, buf, 0, 1, 4, 2, 2), ag(arr, buf, 0, 0, 2, 4, 3),
            ag(arr, buf, 0, 0, 1, 1, 4), ag(arr, buf, 0, 1, 1, 1, 5),
        ]
        for c in out:
            c.start()
        return out

    def ag_relay(arr, buf):
        ag_wait(arr, buf, 2, 0)
        a = ag(arr, buf, 2, 0, 4, 6, 6)
        a.start()
        b = ag(arr, buf, 2, 0, 1, 3, 8)
        b.start()
        ag_wait(arr, buf, 4, 1)
        c = ag(arr, buf, 4, 1, 2, 6, 7)
        c.start()
        d = ag(arr, buf, 4, 1, 1, 5, 9)
        d.start()
        return [a, b, c, d]

    def ag_near(arr, buf):
        ag_wait(arr, buf, 2, 1)
        a = ag(arr, buf, 2, 1, 1, 3, 10)
        a.start()
        ag_wait(arr, buf, 4, 0)
        b = ag(arr, buf, 4, 0, 1, 5, 11)
        b.start()
        return [a, b]

    def ag_far(arr, buf):
        out = []
        for half in range(2):
            ag_wait(arr, buf, 6, half)
            a = ag(arr, buf, 6, half, 1, 7, 12 + half)
            a.start()
            out.append(a)
        return out

    def ag_side(arr, buf, q):
        ag_wait(arr, buf, q, 0)
        ag_wait(arr, buf, q, 1)

    sent = []
    cp_tok.wait()
    sent += ag_own(0, xa)

    sub = lax.broadcasted_iota(jnp.int32, (TOK, TOK), 0)
    lane = lax.broadcasted_iota(jnp.int32, (TOK, TOK), 1)
    lg = nn(xa[0], rw_ref[...])
    logit[...] = lg
    ids = ids_ref[...]
    dense = jnp.zeros((TOK, ROUTED), F32)
    mask = jnp.zeros((TOK, ROUTED), F32)
    total = jnp.zeros((TOK, 1), F32)
    for k in range(4):
        hit = ids[:, k : k + 1] == lane
        value = jnp.exp(jnp.sum(jnp.where(hit, lg, 0.0), axis=1, keepdims=True))
        total = total + value
        dense = jnp.where(hit, value, dense)
        mask = jnp.where(hit, 1.0, mask)
    dense = dense / total
    prob[...] = dense
    before = jnp.where(lane < sub, 1.0, 0.0).astype(BF)
    rank = nn(before, mask.astype(BF))
    rank = jnp.where(mask > 0.5, rank, -1.0)
    meta[0, 0:8, :] = dense.T[0:8]
    meta[0, 8:16, :] = rank.T[0:8]
    meta_sent = []
    for q in range(1, SRC):
        c = pltpu.make_async_remote_copy(
            src_ref=meta.at[0], dst_ref=meta.at[INV[q]], send_sem=mt_s.at[q], recv_sem=mt_r.at[INV[q]],
            device_id=(dp, place[q]), device_id_type=MESH,
        )
        c.start()
        meta_sent.append(c)

    sent += ag_relay(0, xa)
    cp_grad.wait()
    sent += ag_own(1, oa)
    sent += ag_near(0, xa)

    for q in range(1, SRC):
        pltpu.make_async_remote_copy(
            src_ref=meta.at[0], dst_ref=meta.at[q], send_sem=mt_s.at[q], recv_sem=mt_r.at[q],
            device_id=(dp, place[q]), device_id_type=MESH,
        ).wait_recv()

    slot_of = lax.broadcasted_iota(jnp.int32, (CAP, TOK), 0).astype(F32)

    def pick(q):
        return (slot_of == meta[q, pl.ds(8 + ex, 1), :]).astype(F32)

    def gather_tok(q):
        rows = nn(pick(q).astype(BF), xa[q]).astype(BF)
        xr[q * CAP : (q + 1) * CAP, :] = rows

    def gather_grad(q):
        p = pick(q)
        weight = jnp.sum(p * meta[q, pl.ds(ex, 1), :], axis=1, keepdims=True)
        rows = nn(p.astype(BF), oa[q])
        dy[q * CAP : (q + 1) * CAP, :] = (weight * rows).astype(BF)

    for q in (1, 3, 5):
        ag_side(0, xa, q)
    for q in range(6):
        gather_tok(q)
    sent += ag_far(0, xa)
    gather_tok(6)
    ag_side(0, xa, 7)
    gather_tok(7)
    cp_gu.wait()

    def forward(f, _):
        a = pl.ds(pl.multiple_of(f * 256, 256), 256)
        b = pl.ds(pl.multiple_of(FF + f * 256, 256), 256)
        g = nn(xr[...], gu[:, a])
        u = nn(xr[...], gu[:, b])
        s = lax.logistic(g)
        act = g * s
        h = (act * u).astype(BF)
        hid[:, a] = h
        hidt[a, :] = h.T
        pg[:, a] = (u * s * (1.0 + g * (1.0 - s))).astype(BF)
        pg[:, b] = act.astype(BF)
        return 0

    lax.fori_loop(0, 3, forward, 0)
    sent += ag_relay(1, oa)
    lax.fori_loop(3, 6, forward, 0)
    sent += ag_near(1, oa)

    def flip(k, _):
        a = pl.ds(pl.multiple_of(k * 256, 256), 256)
        xt[a, :] = xr[:, a].T
        return 0

    lax.fori_loop(0, D // 256, flip, 0)
    for q in (1, 3, 5):
        ag_side(1, oa, q)
    for q in range(6):
        gather_grad(q)
    sent += ag_far(1, oa)
    gather_grad(6)
    ag_side(1, oa, 7)
    gather_grad(7)
    cp_dn.wait()
    for c in sent:
        c.wait_send()
    for c in meta_sent:
        c.wait_send()

    axes = (((xp, xm, px), (zp, zm, pz)), ((zp, zm, pz), (xp, xm, px)))

    def send1(col, kind, slot, ring, zr):
        plus, minus, fc = axes[col][0]
        base = (
            ((fc + 2) % 4) * 4, ((fc + 2) % 4) * 4 + 2,
            ((fc + 1) % 4) * 4 + 2, ((fc + 3) % 4) * 4,
            ((fc + 1) % 4) * 4, ((fc + 3) % 4) * 4 + 2,
        )[kind]
        return pltpu.make_async_remote_copy(
            src_ref=part.at[ring, col, pl.ds(base, 2), pl.ds(0, zr)],
            dst_ref=r1.at[slot, col, kind, :, pl.ds(0, zr)],
            send_sem=s1.at[slot, col, kind], recv_sem=q1.at[slot, col, kind],
            device_id=(plus if kind % 2 == 0 else minus, ex), device_id_type=MESH,
        )

    def send2(col, kind, slot, ring, zr):
        plus, minus, sc = axes[col][1]
        fc = axes[col][0][2]
        h = zr // 2
        step, low = ((2, 0), (2, h), (1, h), (3, 0), (1, 0), (3, h))[kind]
        return pltpu.make_async_remote_copy(
            src_ref=part.at[ring, col, fc * 4 + (sc + step) % 4, pl.ds(low, h)],
            dst_ref=r2.at[slot, col, kind, pl.ds(0, h)],
            send_sem=s2.at[slot, col, kind], recv_sem=q2.at[slot, col, kind],
            device_id=(plus if kind % 2 == 0 else minus, ex), device_id_type=MESH,
        )

    def f32(v):
        return v.astype(F32)

    def compute(c, lhs, rhs_of, zr):
        slot, ring = c % DEP, c % RING
        rhs = rhs_of(c)
        rows = 4 * zr

        def one(b, _):
            r = nn(lhs[pl.ds(pl.multiple_of(b * rows, rows), rows), :], rhs).astype(BF)
            for k in range(4):
                part[ring, 0, b * 4 + k, 0:zr] = r[k * zr : (k + 1) * zr, 0:128]
                part[ring, 1, k * 4 + b, 0:zr] = r[k * zr : (k + 1) * zr, 128:256]
            return 0

        lax.fori_loop(0, 4, one, 0)
        for kind in range(4):
            for col in range(2):
                send1(col, kind, slot, ring, zr).start()

    def stage1(c, zr):
        slot, ring = c % DEP, c % RING
        for col in range(2):
            fc = axes[col][0][2]
            for kind in range(2):
                send1(col, kind, slot, ring, zr).wait_recv()
                base = ((fc + 1) % 4) * 4 if kind == 0 else ((fc + 3) % 4) * 4 + 2
                at = (ring, col, pl.ds(base, 2), pl.ds(0, zr))
                part[at] = (f32(part[at]) + f32(r1[slot, col, kind, :, 0:zr])).astype(BF)
                send1(col, 4 + kind, slot, ring, zr).start()

    def stage2(c, zr):
        slot, ring = c % DEP, c % RING
        for col in range(2):
            fc = axes[col][0][2]
            for kind in range(2, 6):
                send1(col, kind, slot, ring, zr).wait_recv()
            for half, (a, b) in enumerate(((4, 3), (2, 5))):
                at = (ring, col, pl.ds(fc * 4 + 2 * half, 2), pl.ds(0, zr))
                part[at] = (
                    f32(part[at]) + f32(r1[slot, col, a, :, 0:zr]) + f32(r1[slot, col, b, :, 0:zr])
                ).astype(BF)
            for kind in range(4):
                send1(col, kind, slot, ring, zr).wait_send()
            for kind in range(4):
                send2(col, kind, slot, ring, zr).start()

    def stage3(c, zr):
        slot, ring = c % DEP, c % RING
        h = zr // 2
        for col in range(2):
            fc, sc = axes[col][0][2], axes[col][1][2]
            for kind in range(2):
                send2(col, kind, slot, ring, zr).wait_recv()
                step, low = ((1, 0), (3, h))[kind]
                at = (ring, col, fc * 4 + (sc + step) % 4, pl.ds(low, h))
                part[at] = (f32(part[at]) + f32(r2[slot, col, kind, 0:h])).astype(BF)
                send2(col, 4 + kind, slot, ring, zr).start()
            for kind in range(4, 6):
                send1(col, kind, slot, ring, zr).wait_send()

    def stage4(c, zr, out, first):
        slot, ring = c % DEP, c % RING
        h = zr // 2
        for col in range(2):
            fc, sc = axes[col][0][2], axes[col][1][2]
            for kind in range(2, 6):
                send2(col, kind, slot, ring, zr).wait_recv()
            cols = pl.ds(pl.multiple_of((c - first) * 256 + col * 128, 128), 128)
            for half, (a, b) in enumerate(((4, 3), (2, 5))):
                own = part[ring, col, fc * 4 + sc, half * h : (half + 1) * h]
                out[half * h : (half + 1) * h, cols] = (
                    f32(own) + f32(r2[slot, col, a, 0:h]) + f32(r2[slot, col, b, 0:h])
                ).astype(BF)
            for kind in range(6):
                send2(col, kind, slot, ring, zr).wait_send()

    def both(c, fn, on_down, on_gate):
        @pl.when(jnp.logical_and(c >= 0, c < ND))
        def _():
            fn(c, *on_down)

        @pl.when(jnp.logical_and(c >= ND, c < NC))
        def _():
            fn(c, *on_gate)

    ZD, ZG = FF // 16, D // 16

    def down_rhs(c):
        return dy[:, pl.ds(pl.multiple_of(c * 256, 256), 256)]

    def gate_rhs(c):
        return pg[:, pl.ds(pl.multiple_of((c - ND) * 256, 256), 256)]

    def hidden_grad(f):
        a = pl.ds(pl.multiple_of(f * 256, 256), 256)
        b = pl.ds(pl.multiple_of(FF + f * 256, 256), 256)
        hg = nt(dy[...], dn[a, :])
        score = jnp.sum(f32(hid[:, a]) * hg, axis=1, keepdims=True)
        psum[...] = jnp.where(f == 0, 0.0, psum[...]) + score
        pg[:, a] = (f32(pg[:, a]) * hg).astype(BF)
        pg[:, b] = (f32(pg[:, b]) * hg).astype(BF)

    def ps_copy(q):
        return pltpu.make_async_remote_copy(
            src_ref=psend.at[q], dst_ref=precv.at[INV[q]], send_sem=ps_s.at[q], recv_sem=ps_r.at[INV[q]],
            device_id=(dp, place[q]), device_id_type=MESH,
        )

    def send_scores():
        for q in range(SRC):
            row = jnp.sum(pick(q) * psum[q * CAP : (q + 1) * CAP, :], axis=0, keepdims=True)
            if q == 0:
                precv[0] = jnp.broadcast_to(row, (8, TOK))
            else:
                psend[q] = jnp.broadcast_to(row, (8, TOK))
        for q in range(1, SRC):
            ps_copy(q).start()

    def row_grad(k):
        def one(j, _):
            at = pl.ds(pl.multiple_of((k * 2 + j) * 256, 256), 256)
            rg[:, at] = nt(pg[...], gu[at, :]).astype(BF)
            return 0

        lax.fori_loop(0, 2, one, 0)

    def rt_copy(q):
        return pltpu.make_async_remote_copy(
            src_ref=rg.at[pl.ds(q * CAP, CAP)], dst_ref=rb.at[pl.ds(INV[q] * CAP, CAP)],
            send_sem=rt_s.at[q], recv_sem=rt_r.at[INV[q]],
            device_id=(dp, place[q]), device_id_type=MESH,
        )

    def rt_wait(q):
        pltpu.make_async_remote_copy(
            src_ref=rg.at[pl.ds(q * CAP, CAP)], dst_ref=rb.at[pl.ds(q * CAP, CAP)],
            send_sem=rt_s.at[q], recv_sem=rt_r.at[q],
            device_id=(dp, place[q]), device_id_type=MESH,
        ).wait_recv()

    def send_rows():
        for q in range(1, SRC):
            rt_copy(q).start()
        rb[0:CAP, :] = rg[0:CAP, :]

    def logit_grad():
        for q in range(1, SRC):
            pltpu.make_async_remote_copy(
                src_ref=psend.at[q], dst_ref=precv.at[q], send_sem=ps_s.at[q], recv_sem=ps_r.at[q],
                device_id=(dp, place[q]), device_id_type=MESH,
            ).wait_recv()
        for q in range(1, SRC):
            ps_copy(q).wait_send()
        scores = jnp.zeros((ROUTED, TOK), F32)
        for q in range(SRC):
            scores = jnp.where(sub == place[q], precv[q, 0:1, :], scores)
        scores = scores.T
        mean = jnp.sum(scores, axis=1, keepdims=True)
        z = jnp.sum(jnp.where(sub == lane, z_ref[...], 0.0), axis=1, keepdims=True)
        lgt = logit[...]
        log_total = jnp.log(jnp.sum(jnp.exp(lgt), axis=1, keepdims=True))
        z_grad = 2.0 * z * log_total * jnp.exp(lgt - log_total)
        lg_out[...] = (z_grad + scores - prob[...] * mean).astype(BF)

    def token_grad():
        for q in range(1, SRC):
            rt_wait(q)
        for q in range(1, SRC):
            rt_copy(q).wait_send()
        for q in range(SRC):
            sel[q * CAP : (q + 1) * CAP, :] = (
                slot_of == meta[0, pl.ds(8 + place[q], 1), :]
            ).astype(F32).astype(BF)
        chosen = sel[...]
        grad = lg_out[...]

        def one(k, _):
            at = pl.ds(pl.multiple_of(k * 256, 256), 256)
            tg_out[:, at] = (tn(chosen, rb[:, at]) + nt(grad, rw_ref[at, :])).astype(BF)
            return 0

        lax.fori_loop(0, D // 256, one, 0)

    def body(i, _):
        @pl.when(i < ND)
        def _():
            compute(i, hidt, down_rhs, ZD)

        @pl.when(jnp.logical_and(i >= ND, i < NC))
        def _():
            compute(i, xt, gate_rhs, ZG)

        @pl.when(i < 6)
        def _():
            hidden_grad(i)

        @pl.when(i == 6)
        def _():
            send_scores()

        @pl.when(jnp.logical_and(i >= ND, i < ND + 4))
        def _():
            row_grad(i - ND)

        @pl.when(i == ND + 3)
        def _():
            send_rows()

        @pl.when(i == ND + 4)
        def _():
            logit_grad()

        @pl.when(i == NC)
        def _():
            token_grad()

        c4 = i - LAG4

        @pl.when(jnp.logical_and(c4 >= 0, c4 < ND))
        def _():
            stage4(c4, ZD, dng_out, 0)

        @pl.when(c4 >= ND)
        def _():
            stage4(c4, ZG, gug_out, ND)

        both(i - LAG3, stage3, (ZD,), (ZG,))
        both(i - LAG2, stage2, (ZD,), (ZG,))
        both(i - LAG1, stage1, (ZD,), (ZG,))
        return 0

    lax.fori_loop(0, NC + LAG4, body, 0)


def per_device(tokens, out_grad, z_weight, router_weight, expert_ids, gate_up_weight, down_weight):
    vmem = pl.BlockSpec(memory_space=pltpu.VMEM)
    hbm = pl.BlockSpec(memory_space=pl.ANY)
    dma = pltpu.SemaphoreType.DMA
    token_grad, logit_grad, gate_up_grad, down_grad = pl.pallas_call(
        kernel,
        out_shape=(
            jax.ShapeDtypeStruct((TOK, D), BF),
            jax.ShapeDtypeStruct((TOK, ROUTED), BF),
            jax.ShapeDtypeStruct((D // 16, 2 * FF), BF),
            jax.ShapeDtypeStruct((FF // 16, D), BF),
        ),
        in_specs=[hbm, hbm, vmem, vmem, vmem, hbm, hbm],
        out_specs=(vmem, vmem, vmem, vmem),
        scratch_shapes=[
            pltpu.VMEM((SRC, TOK, D), BF),
            pltpu.VMEM((SRC, TOK, D), BF),
            pltpu.VMEM((SRC, 16, TOK), F32),
            pltpu.VMEM((TOK, ROUTED), F32),
            pltpu.VMEM((TOK, ROUTED), F32),
            pltpu.VMEM((ROWS, D), BF),
            pltpu.VMEM((D, ROWS), BF),
            pltpu.VMEM((ROWS, D), BF),
            pltpu.VMEM((ROWS, FF), BF),
            pltpu.VMEM((FF, ROWS), BF),
            pltpu.VMEM((ROWS, 2 * FF), BF),
            pltpu.VMEM((D, 2 * FF), BF),
            pltpu.VMEM((FF, D), BF),
            pltpu.VMEM((RING, 2, 16, 128, 128), BF),
            pltpu.VMEM((DEP, 2, 6, 2, 128, 128), BF),
            pltpu.VMEM((DEP, 2, 6, 64, 128), BF),
            pltpu.VMEM((ROWS, D), BF),
            pltpu.VMEM((ROWS, D), BF),
            pltpu.VMEM((ROWS, TOK), BF),
            pltpu.VMEM((ROWS, 1), F32),
            pltpu.VMEM((SRC, 8, TOK), F32),
            pltpu.VMEM((SRC, 8, TOK), F32),
            dma((4,)),
            dma((2, 14)), dma((2, SRC, 2)),
            dma((SRC,)), dma((SRC,)),
            dma((SRC,)), dma((SRC,)),
            dma((SRC,)), dma((SRC,)),
            dma((DEP, 2, 6)), dma((DEP, 2, 6)),
            dma((DEP, 2, 6)), dma((DEP, 2, 6)),
        ],
        compiler_params=pltpu.CompilerParams(
            collective_id=0, has_side_effects=True, vmem_limit_bytes=67043328
        ),
        name="moe_backward",
    )(
        tokens, out_grad, z_weight.reshape(1, TOK), router_weight, expert_ids,
        gate_up_weight[0], down_weight[0],
    )
    router_part = lax.dot_general(
        tokens, logit_grad, (((0,), (0,)), ((), ())), preferred_element_type=F32
    )
    router_grad = lax.psum(router_part, ("dp", "expert"))
    return token_grad, router_grad, gate_up_grad[None], down_grad[None]


def solution(mesh):
    return jax.shard_map(
        per_device,
        mesh=mesh,
        in_specs=(
            P(("dp", "expert"), None),
            P(("dp", "expert"), None),
            P(("dp", "expert")),
            P(),
            P(("dp", "expert"), None),
            P("expert", None, None),
            P("expert", None, None),
        ),
        out_specs=(
            P(("dp", "expert"), None),
            P(),
            P("expert", "dp", None),
            P("expert", "dp", None),
        ),
        check_vma=False,
    )
```

time: 321 us -> 330 us (1.028)
  Pallas kernels: 0 us -> 157 us
  matrix products: 54.4 us -> 2.35 us
  waiting for transfers between devices: 180 us -> 145 us
  local copies, waits for them, and re-layouts: 36.3 us -> 9.65 us
  starting transfers between devices: 19.3 us -> 0.04 us
  other arithmetic: 15 us -> 0 us
    pallas_call x0 -> x1, Pallas kernels: none -> 157 us  [per_device(): pl.pallas_call(kernel, out_shape=(jax.ShapeDtypeStruct((TOK, D), BF), jax...]
    dot_general x8 -> x0, matrix products: 53.2 us -> none  [the longest x1 11.3 us: expert_rows(): lax.dot_general(pre_grad, w_gateup, (((1,), (1,)), ((), ())), preferred_e...]
    all_to_all x5 -> x0, waiting for transfers between devices: 47.1 us -> none  [the longest x1 26.4 us: per_device(): lax.all_to_all(send_in.reshape(flight, capacity, width), 'expert', split_...]
    psum x1, waiting for transfers between devices: 119 us -> 145 us  [per_device(): router_grad = lax.psum(router_part, ('dp', 'expert'))]
    gather x8 -> x0, local copies, waits for them, and re-layouts: 19 us -> none  [the longest x2 6.08 us: per_device(): flat_dx[slot_at]]
    all_to_all x5 -> x0, starting transfers between devices: 19 us -> none  [the longest x1 4.71 us: per_device(): lax.all_to_all(send_in.reshape(flight, capacity, width), 'expert', split_...]
    reduce_scatter x2 -> x0, waiting for transfers between devices: 13.9 us -> none  [the longest x1 13.9 us: per_device(): lax.psum_scatter(part_gateup[None], 'dp', scatter_dimension=1, tiled=True)]
    scatter x2 -> x0, local copies, waits for them, and re-layouts: 4.88 us -> none  [the longest x1 2.45 us: per_device(): jnp.zeros((flight * capacity,), jnp.bool_).at[position]]
  transfers between devices with their start and end apart: 8 -> 1, of which waited for: 6 -> 1; matrix products, arithmetic and copies ran while one was open for 20% -> 0% of each run, Pallas kernels for 0% -> 0%
where the time goes in v1:
time: 330 us; the launch traced here: 329 us
  Pallas kernels  157 us (48%)
  waiting for transfers between devices  145 us (44%)
  between operations  14 us (4%)
  local copies, waits for them, and re-layouts  9.65 us (3%)
    pallas_call x1, Pallas kernels, per_device(): pl.pallas_call(kernel, out_shape=(jax.ShapeDtypeStruct((TOK, D), BF), jax...  157 us
    psum x1, waiting for transfers between devices, per_device(): router_grad = lax.psum(router_part, ('dp', 'expert'))  145 us
    unnamed x5, local copies, waits for them, and re-layouts  9.65 us
  transfers between devices with their start and end apart: 1, of which 1 were waited for; matrix products, arithmetic and copies ran while one was open for 0% of the time, Pallas kernels for 0%

profile of v1, /device:TPU:0, one launch (start us, length us, event | category | flops | bytes accessed | tf_op | source)
XLA Modules:
  0.0 328.6 jit_solution(3295584571454695630)
XLA Ops:
  7.2 0.0 all-reduce.2.cloned.1.call-start
  7.2 1.4 copy.11.ids_ref
  8.6 157.2 %moe_backward.1 = (bf16[128,2048]{1,0:T(8,128)(2,1)}, bf16[128,128]{1,0:T(8,128)(2,1)}, bf16[128,3072]{1,0:T(8,128)(2,1)}, bf16[96,2048]{1,0:T(8,128)(2,1)}) custom-call(bf16[128,2048]{1,0:T(8,128)(2,1)} %tokens_hbm.1, bf16[128,2048]{1,0:T(8,128)(2,1)} %grad_hbm.1, f32[1,128]{1,0:T(1,128)} %bitcast.13, bf16[2048,128]{1,0:T(8,128)(2,1)} %rw_ref.1, ...), custom_call_target="tpu_custom_call" | custom-call | tf_op jit(solution)/shard_map/moe_backward/pallas_call | solution.py:512
  165.8 2.4 convolution_bitcast_fusion
  168.2 0.0 all-reduce.2.cloned.1.call-update
  168.2 145.3 %all-reduce.2.cloned.1.call-done = f32[2048,128]{0,1:T(8,128)} async-done(((f32[2048,128]{0,1:T(8,128)}), f32[2048,128]{0,1:T(8,128)}) %all-reduce.2.cloned.1.call-update) | async-done | bytes 1048592 | tf_op jit(solution)/shard_map/psum | solution.py:564
  313.5 2.5 copy.12
  316.1 1.9 copy.17
  317.9 2.1 copy.18
  320.0 1.8 copy.19
Async XLA Ops:
  7.2 306.4 %all-reduce.2.cloned.1.call-start = ((), (), s32[]{:S(2)}) async-start(), calls=%async_computation | async-start | bytes 2097152 | tf_op jit(solution)/shard_map/psum | solution.py:564
Sparse Core Ops, SparseCore 0:
  168.3 145.1 all-reduce.1

commit v2 on v1

--- a/solution.py
+++ b/solution.py
@@ -16,6 +16,7 @@
 D = 2048
 FF = 1536
 SRC = 8
+NDP = 16
 ROWS = SRC * CAP
 ROUTED = 128
 ND = D // 256
@@ -23,7 +24,7 @@
 NC = ND + NG
 LAG1, LAG2, LAG3, LAG4 = 1, 3, 4, 6
 DEP = 6
-RING = 8
+RING = 7
 INV = (0, 1, 4, 5, 2, 3, 6, 7)
 
 
@@ -41,10 +42,10 @@
 
 def kernel(
     tokens_hbm, grad_hbm, z_ref, rw_ref, ids_ref, gu_hbm, dn_hbm,
-    tg_out, lg_out, gug_out, dng_out,
+    tg_out, rt_out, gug_out, dng_out,
     xa, oa, meta, prob, logit, xr, xt, dy, hid, hidt, pg, gu, dn,
-    part, r1, r2, rg, rb, sel, psum, psend, precv,
-    lsem, ag_s, ag_r, mt_s, mt_r, ps_s, ps_r, rt_s, rt_r, s1, q1, s2, q2,
+    part, r1, r2, rg, rb, sel, psum, psend, precv, lgrad, rpart, rin, rsum, rbuf,
+    lsem, ag_s, ag_r, mt_s, mt_r, ps_s, ps_r, rt_s, rt_r, s1, q1, s2, q2, ra_s, ra_r, rs_s, rs_r, rc_s, rc_r, rd_s, rd_r,
 ):
     dp = lax.axis_index("dp")
     ex = lax.axis_index("expert")
@@ -66,11 +67,11 @@
     cp_dn.start()
 
     barrier = pltpu.get_barrier_semaphore()
-    for to in (xp, xm, zp, zm):
-        pl.semaphore_signal(barrier, inc=1, device_id=(to, ex), device_id_type=MESH)
+    for k in range(1, NDP):
+        pl.semaphore_signal(barrier, inc=1, device_id=((dp + k) % NDP, ex), device_id_type=MESH)
     for q in range(1, SRC):
         pl.semaphore_signal(barrier, inc=1, device_id=(dp, place[q]), device_id_type=MESH)
-    pl.semaphore_wait(barrier, 4 + SRC - 1)
+    pl.semaphore_wait(barrier, NDP - 1 + SRC - 1)
 
     def ag(arr, buf, src_q, half, to_q, dst_q, k):
         rows = pl.ds(half * CAP, CAP)
@@ -141,12 +142,14 @@
     lane = lax.broadcasted_iota(jnp.int32, (TOK, TOK), 1)
     lg = nn(xa[0], rw_ref[...])
     logit[...] = lg
-    ids = ids_ref[...]
+    ids = ids_ref[...].astype(F32)
+    ids = jnp.concatenate([ids, ids], axis=0).T
+    lane_f = lane.astype(F32)
     dense = jnp.zeros((TOK, ROUTED), F32)
     mask = jnp.zeros((TOK, ROUTED), F32)
     total = jnp.zeros((TOK, 1), F32)
     for k in range(4):
-        hit = ids[:, k : k + 1] == lane
+        hit = ids[:, k : k + 1] == lane_f
         value = jnp.exp(jnp.sum(jnp.where(hit, lg, 0.0), axis=1, keepdims=True))
         total = total + value
         dense = jnp.where(hit, value, dense)
@@ -433,7 +436,7 @@
         lgt = logit[...]
         log_total = jnp.log(jnp.sum(jnp.exp(lgt), axis=1, keepdims=True))
         z_grad = 2.0 * z * log_total * jnp.exp(lgt - log_total)
-        lg_out[...] = (z_grad + scores - prob[...] * mean).astype(BF)
+        lgrad[...] = (z_grad + scores - prob[...] * mean).astype(BF)
 
     def token_grad():
         for q in range(1, SRC):
@@ -445,7 +448,7 @@
                 slot_of == meta[0, pl.ds(8 + place[q], 1), :]
             ).astype(F32).astype(BF)
         chosen = sel[...]
-        grad = lg_out[...]
+        grad = lgrad[...]
 
         def one(k, _):
             at = pl.ds(pl.multiple_of(k * 256, 256), 256)
@@ -454,6 +457,98 @@
 
         lax.fori_loop(0, D // 256, one, 0)
 
+    def ra_copy(q):
+        return pltpu.make_async_remote_copy(
+            src_ref=rpart.at[place[q]], dst_ref=rin.at[INV[q]], send_sem=ra_s.at[q], recv_sem=ra_r.at[INV[q]],
+            device_id=(dp, place[q]), device_id_type=MESH,
+        )
+
+    def ra_wait(q):
+        pltpu.make_async_remote_copy(
+            src_ref=rpart.at[place[q]], dst_ref=rin.at[q], send_sem=ra_s.at[q], recv_sem=ra_r.at[q],
+            device_id=(dp, place[q]), device_id_type=MESH,
+        ).wait_recv()
+
+    def rs_copy(k):
+        to = (dp + k) % NDP
+        return pltpu.make_async_remote_copy(
+            src_ref=rsum.at[to], dst_ref=rbuf.at[k], send_sem=rs_s.at[k], recv_sem=rs_r.at[k],
+            device_id=(to, ex), device_id_type=MESH,
+        )
+
+    def rc_copy(k):
+        to = (dp + k) % NDP
+        return pltpu.make_async_remote_copy(
+            src_ref=rt_out.at[ex, dp], dst_ref=rt_out.at[ex, dp], send_sem=rc_s.at[k], recv_sem=rc_r.at[k],
+            device_id=(to, ex), device_id_type=MESH,
+        )
+
+    def rc_wait(k):
+        fr = (dp + NDP - k) % NDP
+        pltpu.make_async_remote_copy(
+            src_ref=rt_out.at[ex, fr], dst_ref=rt_out.at[ex, fr], send_sem=rc_s.at[k], recv_sem=rc_r.at[k],
+            device_id=(fr, ex), device_id_type=MESH,
+        ).wait_recv()
+
+    def rd_copy(q):
+        return pltpu.make_async_remote_copy(
+            src_ref=rt_out.at[ex], dst_ref=rt_out.at[ex], send_sem=rd_s.at[q], recv_sem=rd_r.at[INV[q]],
+            device_id=(dp, place[q]), device_id_type=MESH,
+        )
+
+    def rd_wait(q):
+        pltpu.make_async_remote_copy(
+            src_ref=rt_out.at[place[q]], dst_ref=rt_out.at[place[q]], send_sem=rd_s.at[q], recv_sem=rd_r.at[q],
+            device_id=(dp, place[q]), device_id_type=MESH,
+        ).wait_recv()
+
+    def router_a():
+        grad = lgrad[...]
+
+        def one(b, _):
+            at = pl.ds(pl.multiple_of(b * 256, 256), 256)
+            rpart[b] = tn(xa[0, :, at], grad)
+            return 0
+
+        lax.fori_loop(0, SRC, one, 0)
+        for q in range(1, SRC):
+            ra_copy(q).start()
+
+    def router_b():
+        for q in range(1, SRC):
+            ra_wait(q)
+        acc = rpart[ex]
+        for q in range(1, SRC):
+            acc = acc + rin[q]
+        rsum[...] = acc.reshape(NDP, 16, ROUTED)
+        for k in range(1, NDP):
+            rs_copy(k).start()
+
+    def router_c():
+        acc = rsum[dp]
+        for k in range(1, NDP):
+            rs_copy(k).wait_recv()
+            acc = acc + rbuf[k]
+        rt_out[ex, dp] = acc
+        for k in range(1, NDP):
+            rc_copy(k).start()
+
+    def router_d():
+        for k in range(1, NDP):
+            rc_wait(k)
+        for q in range(1, SRC):
+            rd_copy(q).start()
+
+    def router_end():
+        for q in range(1, SRC):
+            rd_wait(q)
+        for q in range(1, SRC):
+            ra_copy(q).wait_send()
+            rd_copy(q).wait_send()
+        for k in range(1, NDP):
+            rs_copy(k).wait_send()
+            rc_copy(k).wait_send()
+
     def body(i, _):
         @pl.when(i < ND)
         def _():
@@ -479,9 +574,11 @@
         def _():
             send_rows()
 
-        @pl.when(i == ND + 4)
-        def _():
-            logit_grad()
+        for at, step in (
+            (ND, logit_grad), (ND, router_a), (ND + 4, router_b), (ND + 6, router_c),
+            (ND + 8, router_d), (NC + 1, router_end),
+        ):
+            pl.when(i == at)(step)
 
         @pl.when(i == NC)
         def _():
@@ -505,15 +602,24 @@
     lax.fori_loop(0, NC + LAG4, body, 0)
 
 
+def write_out(*refs):
+    sem = refs[8]
+    copies = [pltpu.make_async_copy(refs[k], refs[4 + k], sem.at[k]) for k in range(4)]
+    for c in copies:
+        c.start()
+    for c in copies:
+        c.wait()
+
+
 def per_device(tokens, out_grad, z_weight, router_weight, expert_ids, gate_up_weight, down_weight):
     vmem = pl.BlockSpec(memory_space=pltpu.VMEM)
     hbm = pl.BlockSpec(memory_space=pl.ANY)
     dma = pltpu.SemaphoreType.DMA
-    token_grad, logit_grad, gate_up_grad, down_grad = pl.pallas_call(
+    outs = pl.pallas_call(
         kernel,
         out_shape=(
             jax.ShapeDtypeStruct((TOK, D), BF),
-            jax.ShapeDtypeStruct((TOK, ROUTED), BF),
+            jax.ShapeDtypeStruct((SRC, NDP, 16, ROUTED), F32),
             jax.ShapeDtypeStruct((D // 16, 2 * FF), BF),
             jax.ShapeDtypeStruct((FF // 16, D), BF),
         ),
@@ -542,6 +648,11 @@
             pltpu.VMEM((ROWS, 1), F32),
             pltpu.VMEM((SRC, 8, TOK), F32),
             pltpu.VMEM((SRC, 8, TOK), F32),
+            pltpu.VMEM((TOK, ROUTED), BF),
+            pltpu.VMEM((SRC, D // SRC, ROUTED), F32),
+            pltpu.VMEM((SRC, D // SRC, ROUTED), F32),
+            pltpu.VMEM((NDP, 16, ROUTED), F32),
+            pltpu.VMEM((NDP, 16, ROUTED), F32),
             dma((4,)),
             dma((2, 14)), dma((2, SRC, 2)),
             dma((SRC,)), dma((SRC,)),
@@ -549,20 +660,29 @@
             dma((SRC,)), dma((SRC,)),
             dma((DEP, 2, 6)), dma((DEP, 2, 6)),
             dma((DEP, 2, 6)), dma((DEP, 2, 6)),
+            dma((SRC,)), dma((SRC,)),
+            dma((NDP,)), dma((NDP,)),
+            dma((NDP,)), dma((NDP,)),
+            dma((SRC,)), dma((SRC,)),
         ],
         compiler_params=pltpu.CompilerParams(
             collective_id=0, has_side_effects=True, vmem_limit_bytes=67043328
         ),
         name="moe_backward",
     )(
-        tokens, out_grad, z_weight.reshape(1, TOK), router_weight, expert_ids,
+        tokens, out_grad, z_weight.reshape(1, TOK), router_weight, expert_ids.T,
         gate_up_weight[0], down_weight[0],
     )
-    router_part = lax.dot_general(
-        tokens, logit_grad, (((0,), (0,)), ((), ())), preferred_element_type=F32
-    )
-    router_grad = lax.psum(router_part, ("dp", "expert"))
-    return token_grad, router_grad, gate_up_grad[None], down_grad[None]
+    shapes = tuple(jax.ShapeDtypeStruct(o.shape, o.dtype) for o in outs)
+    token_grad, router_grad, gate_up_grad, down_grad = pl.pallas_call(
+        write_out,
+        out_shape=shapes,
+        in_specs=[vmem] * 4,
+        out_specs=[hbm] * 4,
+        scratch_shapes=[dma((4,))],
+        name="write_out",
+    )(*outs)
+    return token_grad, router_grad.reshape(D, ROUTED), gate_up_grad[None], down_grad[None]
 
 
 def solution(mesh):

time: 330 us -> 167 us (0.51)
  waiting for transfers between devices: 145 us -> 0 us
  between operations: 14 us -> 0.64 us
  local copies, waits for them, and re-layouts: 9.65 us -> 0 us
  Pallas kernels: 157 us -> 166 us
    psum x1 -> x0, waiting for transfers between devices: 145 us -> none  [per_device(): router_grad = lax.psum(router_part, ('dp', 'expert'))]
    unnamed x5 -> x0, local copies, waits for them, and re-layouts: 9.65 us -> none
    pallas_call x1, Pallas kernels: 157 us -> 163 us  [per_device(): pl.pallas_call(kernel, out_shape=(jax.ShapeDtypeStruct((TOK, D), BF), jax...]
  transfers between devices with their start and end apart: 1 -> 0, of which waited for: 1 -> 0; matrix products, arithmetic and copies ran while one was open for 0% -> 0% of each run, Pallas kernels for 0% -> 0%
where the time goes in v2:
time: 167 us
  Pallas kernels  166 us (99%)
    pallas_call x1, Pallas kernels, per_device(): pl.pallas_call(kernel, out_shape=(jax.ShapeDtypeStruct((TOK, D), BF), jax...  163 us

profile of v2, /device:TPU:0, one launch (start us, length us, event | category | flops | bytes accessed | tf_op | source)
XLA Modules:
  0.0 166.9 jit_solution(13546214207130148469)
XLA Ops:
  0.6 163.0 %moe_backward.1 = (bf16[128,2048]{1,0:T(8,128)(2,1)}, f32[8,16,16,128]{3,2,1,0:T(8,128)}, bf16[128,3072]{1,0:T(8,128)(2,1)}, bf16[96,2048]{1,0:T(8,128)(2,1)}) custom-call(bf16[128,2048]{1,0:T(8,128)(2,1)} %tokens_hbm.1, bf16[128,2048]{1,0:T(8,128)(2,1)} %grad_hbm.1, f32[1,128]{1,0:T(1,128)} %bitcast.10, bf16[2048,128]{1,0:T(8,128)(2,1)} %rw_ref.1, ...), custom_call_target="tpu_custom_call" | custom-call | tf_op jit(solution)/shard_map/moe_backward/pallas_call | solution.py:618
  163.7 3.3 %write_out.1 = (bf16[128,2048]{1,0:T(8,128)(2,1)}, f32[8,16,16,128]{3,2,1,0:T(8,128)}, bf16[128,3072]{1,0:T(8,128)(2,1)}, bf16[96,2048]{1,0:T(8,128)(2,1)}) custom-call(bf16[128,2048]{1,0:T(8,128)(2,1)} %get-tuple-element.12.refs_0_, f32[8,16,16,128]{3,2,1,0:T(8,128)} %get-tuple-element.13.refs_1_, bf16[128,3072]{1,0:T(8,128)(2,1)} %get-tuple-element.14.refs_2_, ...), custom_call_target="tpu_custom_call" | custom-call | tf_op jit(solution)/shard_map/write_out/pallas_call | solution.py:677

commit v3 on v2

--- a/solution.py
+++ b/solution.py
@@ -25,6 +25,7 @@
 LAG1, LAG2, LAG3, LAG4 = 1, 3, 4, 6
 DEP = 6
 RING = 7
+CUTS = (0, 256, 512, 1024, 1536, 2048)
 INV = (0, 1, 4, 5, 2, 3, 6, 7)
 
 
@@ -44,15 +45,21 @@
     tokens_hbm, grad_hbm, z_ref, rw_ref, ids_ref, gu_hbm, dn_hbm,
     tg_out, rt_out, gug_out, dng_out,
     xa, oa, meta, prob, logit, xr, xt, dy, hid, hidt, pg, gu, dn,
-    part, r1, r2, rg, rb, sel, psum, psend, precv, lgrad, rpart, rin, rsum, rbuf,
-    lsem, ag_s, ag_r, mt_s, mt_r, ps_s, ps_r, rt_s, rt_r, s1, q1, s2, q2, ra_s, ra_r, rs_s, rs_r, rc_s, rc_r, rd_s, rd_r,
+    part, r1, r2, rg, rb, sel, psum, psend, precv, lgrad, rpart, rin, rsum, rbufz, rsumx, rbufx,
+    lsem, ag_s, ag_r, mt_s, mt_r, ps_s, ps_r, rt_s, rt_r, s1, q1, s2, q2, ra_s, ra_r, rs_s, rs_r, rd_s, rd_r,
 ):
     dp = lax.axis_index("dp")
     ex = lax.axis_index("expert")
     px, pz = dp // 4, dp % 4
     py, pc = ex // 2, ex % 2
-    xp, xm = ((px + 1) % 4) * 4 + pz, ((px + 3) % 4) * 4 + pz
-    zp, zm = px * 4 + (pz + 1) % 4, px * 4 + (pz + 3) % 4
+
+    def xs(k):
+        return ((px + k) % 4) * 4 + pz
+
+    def zs(k):
+        return px * 4 + (pz + k) % 4
+
+    xp, xm, zp, zm = xs(1), xs(3), zs(1), zs(3)
     yp, ym, yo = (py + 1) % 4, (py + 3) % 4, (py + 2) % 4
     oc = 1 - pc
     place = (ex, py * 2 + oc, ym * 2 + pc, ym * 2 + oc, yp * 2 + pc, yp * 2 + oc, yo * 2 + pc, yo * 2 + oc)
@@ -67,76 +74,69 @@
     cp_dn.start()
 
     barrier = pltpu.get_barrier_semaphore()
-    for k in range(1, NDP):
-        pl.semaphore_signal(barrier, inc=1, device_id=((dp + k) % NDP, ex), device_id_type=MESH)
+    for k in range(1, 4):
+        pl.semaphore_signal(barrier, inc=1, device_id=(xs(k), ex), device_id_type=MESH)
+        pl.semaphore_signal(barrier, inc=1, device_id=(zs(k), ex), device_id_type=MESH)
     for q in range(1, SRC):
         pl.semaphore_signal(barrier, inc=1, device_id=(dp, place[q]), device_id_type=MESH)
-    pl.semaphore_wait(barrier, NDP - 1 + SRC - 1)
-
-    def ag(arr, buf, src_q, half, to_q, dst_q, k):
+    pl.semaphore_wait(barrier, 6 + SRC - 1)
+
+    OWN = ((0, 0, 4, 2), (0, 1, 2, 4), (0, 1, 4, 2), (0, 0, 2, 4), (0, 0, 1, 1), (0, 1, 1, 1))
+    RELAY = ((2, 0, 4, 6), (2, 0, 1, 3), (4, 1, 2, 6), (4, 1, 1, 5))
+    NEAR = ((2, 1, 1, 3), (4, 0, 1, 5))
+    FAR = ((6, 0, 1, 7), (6, 1, 1, 7))
+    ALL = OWN + RELAY + NEAR + FAR
+
+    def ag_view(part_no, q, half):
         rows = pl.ds(half * CAP, CAP)
-        return pltpu.make_async_remote_copy(
-            src_ref=buf.at[src_q, rows], dst_ref=buf.at[dst_q, rows],
-            send_sem=ag_s.at[arr, k], recv_sem=ag_r.at[arr, dst_q, half],
+        if part_no == 0:
+            return xa.at[q, rows]
+        return oa.at[q, rows, pl.ds(CUTS[part_no - 1], CUTS[part_no] - CUTS[part_no - 1])]
+
+    def ag(part_no, copy):
+        src_q, half, to_q, dst_q = copy
+        return pltpu.make_async_remote_copy(
+            src_ref=ag_view(part_no, src_q, half), dst_ref=ag_view(part_no, dst_q, half),
+            send_sem=ag_s.at[part_no, ALL.index(copy)], recv_sem=ag_r.at[part_no, dst_q, half],
             device_id=(dp, place[to_q]), device_id_type=MESH,
         )
 
-    def ag_wait(arr, buf, q, half):
-        rows = pl.ds(half * CAP, CAP)
+    def ag_wait(part_no, q, half):
         pltpu.make_async_remote_copy(
-            src_ref=buf.at[q, rows], dst_ref=buf.at[q, rows],
-            send_sem=ag_s.at[arr, 0], recv_sem=ag_r.at[arr, q, half],
+            src_ref=ag_view(part_no, q, half), dst_ref=ag_view(part_no, q, half),
+            send_sem=ag_s.at[part_no, 0], recv_sem=ag_r.at[part_no, q, half],
             device_id=(dp, place[1]), device_id_type=MESH,
         ).wait_recv()
 
-    def ag_own(arr, buf):
-        out = [
-            ag(arr, buf, 0, 0, 4, 2, 0), ag(arr, buf, 0, 1, 2, 4, 1),
-            ag(arr, buf, 0, 1, 4, 2, 2), ag(arr, buf, 0, 0, 2, 4, 3),
-            ag(arr, buf, 0, 0, 1, 1, 4), ag(arr, buf, 0, 1, 1, 1, 5),
-        ]
-        for c in out:
-            c.start()
-        return out
-
-    def ag_relay(arr, buf):
-        ag_wait(arr, buf, 2, 0)
-        a = ag(arr, buf, 2, 0, 4, 6, 6)
-        a.start()
-        b = ag(arr, buf, 2, 0, 1, 3, 8)
-        b.start()
-        ag_wait(arr, buf, 4, 1)
-        c = ag(arr, buf, 4, 1, 2, 6, 7)
-        c.start()
-        d = ag(arr, buf, 4, 1, 1, 5, 9)
-        d.start()
-        return [a, b, c, d]
-
-    def ag_near(arr, buf):
-        ag_wait(arr, buf, 2, 1)
-        a = ag(arr, buf, 2, 1, 1, 3, 10)
-        a.start()
-        ag_wait(arr, buf, 4, 0)
-        b = ag(arr, buf, 4, 0, 1, 5, 11)
-        b.start()
-        return [a, b]
-
-    def ag_far(arr, buf):
-        out = []
+    def ag_own(part_no):
+        for c in OWN:
+            ag(part_no, c).start()
+
+    def ag_relay(part_no):
+        ag_wait(part_no, 2, 0)
+        ag(part_no, RELAY[0]).start()
+        ag(part_no, RELAY[1]).start()
+        ag_wait(part_no, 4, 1)
+        ag(part_no, RELAY[2]).start()
+        ag(part_no, RELAY[3]).start()
+
+    def ag_near(part_no):
+        ag_wait(part_no, 2, 1)
+        ag(part_no, NEAR[0]).start()
+        ag_wait(part_no, 4, 0)
+        ag(part_no, NEAR[1]).start()
+
+    def ag_far(part_no):
         for half in range(2):
-            ag_wait(arr, buf, 6, half)
-            a = ag(arr, buf, 6, half, 1, 7, 12 + half)
-            a.start()
-            out.append(a)
-        return out
-
-    def ag_side(arr, buf, q):
-        ag_wait(arr, buf, q, 0)
-        ag_wait(arr, buf, q, 1)
-
-    sent = []
+            ag_wait(part_no, 6, half)
+            ag(part_no, FAR[half]).start()
+
+    def ag_side(part_no, q):
+        ag_wait(part_no, q, 0)
+        ag_wait(part_no, q, 1)
+
     cp_tok.wait()
-    sent += ag_own(0, xa)
+    ag_own(0)
 
     sub = lax.broadcasted_iota(jnp.int32, (TOK, TOK), 0)
     lane = lax.broadcasted_iota(jnp.int32, (TOK, TOK), 1)
@@ -170,10 +170,11 @@
         c.start()
         meta_sent.append(c)
 
-    sent += ag_relay(0, xa)
     cp_grad.wait()
-    sent += ag_own(1, oa)
-    sent += ag_near(0, xa)
+    ag_own(1)
+    ag_relay(0)
+    ag_own(2)
+    ag_near(0)
 
     for q in range(1, SRC):
         pltpu.make_async_remote_copy(
@@ -190,60 +191,70 @@
         rows = nn(pick(q).astype(BF), xa[q]).astype(BF)
         xr[q * CAP : (q + 1) * CAP, :] = rows
 
-    def gather_grad(q):
+    def gather_grad(q, part_no):
         p = pick(q)
         weight = jnp.sum(p * meta[q, pl.ds(ex, 1), :], axis=1, keepdims=True)
-        rows = nn(p.astype(BF), oa[q])
-        dy[q * CAP : (q + 1) * CAP, :] = (weight * rows).astype(BF)
-
+        cols = slice(CUTS[part_no - 1], CUTS[part_no])
+        rows = nn(p.astype(BF), oa[q, :, cols])
+        dy[q * CAP : (q + 1) * CAP, cols] = (weight * rows).astype(BF)
+
+    def grad_near(part_no):
+        for q in (1, 3, 5):
+            ag_side(part_no, q)
+        for q in range(6):
+            gather_grad(q, part_no)
+
+    def grad_far(part_no):
+        ag_far(part_no)
+        gather_grad(6, part_no)
+        ag_side(part_no, 7)
+        gather_grad(7, part_no)
+
+    def grad_part(part_no):
+        grad_near(part_no)
+        grad_far(part_no)
+
+    def forward(lo, hi):
+        def run(f, _):
+            a = pl.ds(pl.multiple_of(f * 256, 256), 256)
+            b = pl.ds(pl.multiple_of(FF + f * 256, 256), 256)
+            g = nn(xr[lo:hi, :], gu[:, a])
+            u = nn(xr[lo:hi, :], gu[:, b])
+            s = lax.logistic(g)
+            act = g * s
+            h = (act * u).astype(BF)
+            hid[lo:hi, a] = h
+            hidt[a, lo:hi] = h.T
+            pg[lo:hi, a] = (u * s * (1.0 + g * (1.0 - s))).astype(BF)
+            pg[lo:hi, b] = act.astype(BF)
+            return 0
+
+        return run
+
+    near, far = forward(0, 6 * CAP), forward(6 * CAP, ROWS)
     for q in (1, 3, 5):
-        ag_side(0, xa, q)
+        ag_side(0, q)
     for q in range(6):
         gather_tok(q)
-    sent += ag_far(0, xa)
+    cp_gu.wait()
+    lax.fori_loop(0, 6, near, 0)
+    ag_relay(1)
+    ag_own(3)
+    ag_far(0)
     gather_tok(6)
-    ag_side(0, xa, 7)
+    ag_near(1)
+    ag_side(0, 7)
     gather_tok(7)
-    cp_gu.wait()
-
-    def forward(f, _):
-        a = pl.ds(pl.multiple_of(f * 256, 256), 256)
-        b = pl.ds(pl.multiple_of(FF + f * 256, 256), 256)
-        g = nn(xr[...], gu[:, a])
-        u = nn(xr[...], gu[:, b])
-        s = lax.logistic(g)
-        act = g * s
-        h = (act * u).astype(BF)
-        hid[:, a] = h
-        hidt[a, :] = h.T
-        pg[:, a] = (u * s * (1.0 + g * (1.0 - s))).astype(BF)
-        pg[:, b] = act.astype(BF)
-        return 0
-
-    lax.fori_loop(0, 3, forward, 0)
-    sent += ag_relay(1, oa)
-    lax.fori_loop(3, 6, forward, 0)
-    sent += ag_near(1, oa)
-
-    def flip(k, _):
+    lax.fori_loop(0, 3, far, 0)
+    ag_relay(2)
+    lax.fori_loop(3, 6, far, 0)
+    ag_near(2)
+    grad_part(1)
+    cp_dn.wait()
+
+    def flip(k):
         a = pl.ds(pl.multiple_of(k * 256, 256), 256)
         xt[a, :] = xr[:, a].T
-        return 0
-
-    lax.fori_loop(0, D // 256, flip, 0)
-    for q in (1, 3, 5):
-        ag_side(1, oa, q)
-    for q in range(6):
-        gather_grad(q)
-    sent += ag_far(1, oa)
-    gather_grad(6)
-    ag_side(1, oa, 7)
-    gather_grad(7)
-    cp_dn.wait()
-    for c in sent:
-        c.wait_send()
-    for c in meta_sent:
-        c.wait_send()
 
     axes = (((xp, xm, px), (zp, zm, pz)), ((zp, zm, pz), (xp, xm, px)))
 
@@ -393,31 +404,32 @@
             ps_copy(q).start()
 
     def row_grad(k):
-        def one(j, _):
-            at = pl.ds(pl.multiple_of((k * 2 + j) * 256, 256), 256)
-            rg[:, at] = nt(pg[...], gu[at, :]).astype(BF)
-            return 0
-
-        lax.fori_loop(0, 2, one, 0)
-
-    def rt_copy(q):
-        return pltpu.make_async_remote_copy(
-            src_ref=rg.at[pl.ds(q * CAP, CAP)], dst_ref=rb.at[pl.ds(INV[q] * CAP, CAP)],
-            send_sem=rt_s.at[q], recv_sem=rt_r.at[INV[q]],
+        at = pl.ds(pl.multiple_of(k * 256, 256), 256)
+        rg[:, at] = nt(pg[...], gu[at, :]).astype(BF)
+
+    HALF = D // 2
+
+    def rt_copy(q, half):
+        cols = pl.ds(half * HALF, HALF)
+        return pltpu.make_async_remote_copy(
+            src_ref=rg.at[pl.ds(q * CAP, CAP), cols], dst_ref=rb.at[pl.ds(INV[q] * CAP, CAP), cols],
+            send_sem=rt_s.at[half, q], recv_sem=rt_r.at[half, INV[q]],
             device_id=(dp, place[q]), device_id_type=MESH,
         )
 
-    def rt_wait(q):
+    def rt_wait(q, half):
+        cols = pl.ds(half * HALF, HALF)
         pltpu.make_async_remote_copy(
-            src_ref=rg.at[pl.ds(q * CAP, CAP)], dst_ref=rb.at[pl.ds(q * CAP, CAP)],
-            send_sem=rt_s.at[q], recv_sem=rt_r.at[q],
+            src_ref=rg.at[pl.ds(q * CAP, CAP), cols], dst_ref=rb.at[pl.ds(q * CAP, CAP), cols],
+            send_sem=rt_s.at[half, q], recv_sem=rt_r.at[half, q],
             device_id=(dp, place[q]), device_id_type=MESH,
         ).wait_recv()
 
-    def send_rows():
-        for q in range(1, SRC):
-            rt_copy(q).start()
-        rb[0:CAP, :] = rg[0:CAP, :]
+    def send_rows(half):
+        for q in range(1, SRC):
+            rt_copy(q, half).start()
+        cols = slice(half * HALF, (half + 1) * HALF)
+        rb[0:CAP, cols] = rg[0:CAP, cols]
 
     def logit_grad():
         for q in range(1, SRC):
@@ -438,15 +450,16 @@
         z_grad = 2.0 * z * log_total * jnp.exp(lgt - log_total)
         lgrad[...] = (z_grad + scores - prob[...] * mean).astype(BF)
 
-    def token_grad():
-        for q in range(1, SRC):
-            rt_wait(q)
-        for q in range(1, SRC):
-            rt_copy(q).wait_send()
-        for q in range(SRC):
-            sel[q * CAP : (q + 1) * CAP, :] = (
-                slot_of == meta[0, pl.ds(8 + place[q], 1), :]
-            ).astype(F32).astype(BF)
+    def token_grad(half):
+        for q in range(1, SRC):
+            rt_wait(q, half)
+        for q in range(1, SRC):
+            rt_copy(q, half).wait_send()
+        if half == 0:
+            for q in range(SRC):
+                sel[q * CAP : (q + 1) * CAP, :] = (
+                    slot_of == meta[0, pl.ds(8 + place[q], 1), :]
+                ).astype(F32).astype(BF)
         chosen = sel[...]
         grad = lgrad[...]
 
@@ -455,7 +468,7 @@
             tg_out[:, at] = (tn(chosen, rb[:, at]) + nt(grad, rw_ref[at, :])).astype(BF)
             return 0
 
-        lax.fori_loop(0, D // 256, one, 0)
+        lax.fori_loop(half * 4, half * 4 + 4, one, 0)
 
     def ra_copy(q):
         return pltpu.make_async_remote_copy(
@@ -469,37 +482,55 @@
             device_id=(dp, place[q]), device_id_type=MESH,
         ).wait_recv()
 
-    def rs_copy(k):
-        to = (dp + k) % NDP
-        return pltpu.make_async_remote_copy(
-            src_ref=rsum.at[to], dst_ref=rbuf.at[k], send_sem=rs_s.at[k], recv_sem=rs_r.at[k],
-            device_id=(to, ex), device_id_type=MESH,
-        )
-
-    def rc_copy(k):
-        to = (dp + k) % NDP
-        return pltpu.make_async_remote_copy(
-            src_ref=rt_out.at[ex, dp], dst_ref=rt_out.at[ex, dp], send_sem=rc_s.at[k], recv_sem=rc_r.at[k],
-            device_id=(to, ex), device_id_type=MESH,
-        )
-
-    def rc_wait(k):
-        fr = (dp + NDP - k) % NDP
+    c1, c2 = pz + pc * (px - pz), px + pc * (pz - px)
+
+    def to1(k):
+        return zs(k) + pc * (xs(k) - zs(k))
+
+    def to2(k):
+        return xs(k) + pc * (zs(k) - xs(k))
+
+    def rsz(k):
+        return pltpu.make_async_remote_copy(
+            src_ref=rsum.at[:, (c1 + k) % 4], dst_ref=rbufz.at[k], send_sem=rs_s.at[0, k], recv_sem=rs_r.at[0, k],
+            device_id=(to1(k), ex), device_id_type=MESH,
+        )
+
+    def rsx(k):
+        return pltpu.make_async_remote_copy(
+            src_ref=rsumx.at[(c2 + k) % 4], dst_ref=rbufx.at[k], send_sem=rs_s.at[1, k], recv_sem=rs_r.at[1, k],
+            device_id=(to2(k), ex), device_id_type=MESH,
+        )
+
+    def rcx(k, at):
+        block = rt_out.at[ex, at, c1]
+        return pltpu.make_async_remote_copy(
+            src_ref=block, dst_ref=block, send_sem=rs_s.at[2, k], recv_sem=rs_r.at[2, k],
+            device_id=(to2(k), ex), device_id_type=MESH,
+        )
+
+    def rcz(k, at):
+        block = rt_out.at[ex, :, at]
+        return pltpu.make_async_remote_copy(
+            src_ref=block, dst_ref=block, send_sem=rs_s.at[3, k], recv_sem=rs_r.at[3, k],
+            device_id=(to1(k), ex), device_id_type=MESH,
+        )
+
+    SAME = (2, 4, 6)
+
+    def rd_copy(q, to_q):
+        block = rt_out.at[place[q]]
+        return pltpu.make_async_remote_copy(
+            src_ref=block, dst_ref=block, send_sem=rd_s.at[q, to_q],
+            recv_sem=rd_r.at[INV[to_q] if to_q != 1 else q + 1],
+            device_id=(dp, place[to_q]), device_id_type=MESH,
+        )
+
+    def rd_wait(q):
+        block = rt_out.at[place[q]]
         pltpu.make_async_remote_copy(
-            src_ref=rt_out.at[ex, fr], dst_ref=rt_out.at[ex, fr], send_sem=rc_s.at[k], recv_sem=rc_r.at[k],
-            device_id=(fr, ex), device_id_type=MESH,
-        ).wait_recv()
-
-    def rd_copy(q):
-        return pltpu.make_async_remote_copy(
-            src_ref=rt_out.at[ex], dst_ref=rt_out.at[ex], send_sem=rd_s.at[q], recv_sem=rd_r.at[INV[q]],
-            device_id=(dp, place[q]), device_id_type=MESH,
-        )
-
-    def rd_wait(q):
-        pltpu.make_async_remote_copy(
-            src_ref=rt_out.at[place[q]], dst_ref=rt_out.at[place[q]], send_sem=rd_s.at[q], recv_sem=rd_r.at[q],
-            device_id=(dp, place[q]), device_id_type=MESH,
+            src_ref=block, dst_ref=block, send_sem=rd_s.at[0, 1], recv_sem=rd_r.at[q],
+            device_id=(dp, place[1]), device_id_type=MESH,
         ).wait_recv()
 
     def router_a():
@@ -507,7 +538,7 @@
 
         def one(b, _):
             at = pl.ds(pl.multiple_of(b * 256, 256), 256)
-            rpart[b] = tn(xa[0, :, at], grad)
+            rpart[b] = tn(xa[0, :, at], grad).astype(BF)
             return 0
 
         lax.fori_loop(0, SRC, one, 0)
@@ -517,37 +548,63 @@
     def router_b():
         for q in range(1, SRC):
             ra_wait(q)
-        acc = rpart[ex]
-        for q in range(1, SRC):
-            acc = acc + rin[q]
-        rsum[...] = acc.reshape(NDP, 16, ROUTED)
-        for k in range(1, NDP):
-            rs_copy(k).start()
+        acc = f32(rpart[ex])
+        for q in range(1, SRC):
+            acc = acc + f32(rin[q])
+        rsum[...] = acc.reshape(4, 4, 16, ROUTED).astype(BF)
+        for k in range(1, 4):
+            rsz(k).start()
 
     def router_c():
-        acc = rsum[dp]
-        for k in range(1, NDP):
-            rs_copy(k).wait_recv()
-            acc = acc + rbuf[k]
-        rt_out[ex, dp] = acc
-        for k in range(1, NDP):
-            rc_copy(k).start()
+        acc = f32(rsum[:, c1])
+        for k in range(1, 4):
+            rsz(k).wait_recv()
+            acc = acc + f32(rbufz[k])
+        rsumx[...] = acc.astype(BF)
+        for k in range(1, 4):
+            rsx(k).start()
+
+    def router_x():
+        acc = f32(rsumx[c2])
+        for k in range(1, 4):
+            rsx(k).wait_recv()
+            acc = acc + f32(rbufx[k])
+        rt_out[ex, c2, c1] = acc
+        for k in range(1, 4):
+            rcx(k, c2).start()
+
+    def router_z():
+        for k in range(1, 4):
+            rcx(k, (c2 + 4 - k) % 4).wait_recv()
+        for k in range(1, 4):
+            rcz(k, c1).start()
 
     def router_d():
-        for k in range(1, NDP):
-            rc_wait(k)
-        for q in range(1, SRC):
-            rd_copy(q).start()
+        for k in range(1, 4):
+            rcz(k, (c1 + 4 - k) % 4).wait_recv()
+        for to_q in SAME:
+            rd_copy(0, to_q).start()
+        rd_copy(0, 1).start()
+
+    def router_e():
+        for q in SAME:
+            rd_wait(q)
+            rd_copy(q, 1).start()
 
     def router_end():
-        for q in range(1, SRC):
+        for q in (1, 3, 5, 7):
             rd_wait(q)
         for q in range(1, SRC):
             ra_copy(q).wait_send()
-            rd_copy(q).wait_send()
-        for k in range(1, NDP):
-            rs_copy(k).wait_send()
-            rc_copy(k).wait_send()
+        for to_q in SAME:
+            rd_copy(0, to_q).wait_send()
+        for q in (0,) + SAME:
+            rd_copy(q, 1).wait_send()
+        for k in range(1, 4):
+            rsz(k).wait_send()
+            rsx(k).wait_send()
+            rcx(k, c2).wait_send()
+            rcz(k, c1).wait_send()
 
     def body(i, _):
         @pl.when(i < ND)
@@ -558,31 +615,59 @@
         def _():
             compute(i, xt, gate_rhs, ZG)
 
-        @pl.when(i < 6)
-        def _():
-            hidden_grad(i)
-
-        @pl.when(i == 6)
+        def parts(k):
+            if k == 0:
+                ag_relay(3)
+                ag_own(4)
+                grad_part(2)
+            elif k == 1:
+                ag_near(3)
+                grad_part(3)
+                ag_relay(4)
+                ag_own(5)
+            elif k == 2:
+                ag_near(4)
+            elif k == 3:
+                grad_part(4)
+                ag_relay(5)
+            elif k == 4:
+                ag_near(5)
+                grad_part(5)
+            else:
+                for n in range(6):
+                    for c in ALL:
+                        ag(n, c).wait_send()
+                for c in meta_sent:
+                    c.wait_send()
+
+        for k in range(6):
+            pl.when(i == k)(functools.partial(parts, k))
+
+        @pl.when(jnp.logical_and(i >= 5, i < 8))
+        def _():
+            hidden_grad(2 * i - 10)
+            hidden_grad(2 * i - 9)
+
+        @pl.when(i < 8)
+        def _():
+            flip(i)
+
+        @pl.when(i == 7)
         def _():
             send_scores()
 
         @pl.when(jnp.logical_and(i >= ND, i < ND + 4))
         def _():
-            row_grad(i - ND)
-
-        @pl.when(i == ND + 3)
-        def _():
-            send_rows()
+            row_grad(2 * (i - ND))
+            row_grad(2 * (i - ND) + 1)
 
         for at, step in (
-            (ND, logit_grad), (ND, router_a), (ND + 4, router_b), (ND + 6, router_c),
-            (ND + 8, router_d), (NC + 1, router_end),
+            (ND, logit_grad), (ND, router_a), (ND + 4, router_b), (ND + 5, router_c),
+            (ND + 6, router_x), (ND + 7, router_z), (ND + 8, router_d), (NC - 1, router_e), (NC + 1, router_end),
+            (ND + 1, functools.partial(send_rows, 0)), (ND + 3, functools.partial(send_rows, 1)),
+            (NC - 3, functools.partial(token_grad, 0)), (NC - 1, functools.partial(token_grad, 1)),
         ):
             pl.when(i == at)(step)
-
-        @pl.when(i == NC)
-        def _():
-            token_grad()
 
         c4 = i - LAG4
 
@@ -619,7 +704,7 @@
         kernel,
         out_shape=(
             jax.ShapeDtypeStruct((TOK, D), BF),
-            jax.ShapeDtypeStruct((SRC, NDP, 16, ROUTED), F32),
+            jax.ShapeDtypeStruct((SRC, 4, 4, 16, ROUTED), F32),
             jax.ShapeDtypeStruct((D // 16, 2 * FF), BF),
             jax.ShapeDtypeStruct((FF // 16, D), BF),
         ),
@@ -649,21 +734,22 @@
             pltpu.VMEM((SRC, 8, TOK), F32),
             pltpu.VMEM((SRC, 8, TOK), F32),
             pltpu.VMEM((TOK, ROUTED), BF),
-            pltpu.VMEM((SRC, D // SRC, ROUTED), F32),
-            pltpu.VMEM((SRC, D // SRC, ROUTED), F32),
-            pltpu.VMEM((NDP, 16, ROUTED), F32),
-            pltpu.VMEM((NDP, 16, ROUTED), F32),
+            pltpu.VMEM((SRC, D // SRC, ROUTED), BF),
+            pltpu.VMEM((SRC, D // SRC, ROUTED), BF),
+            pltpu.VMEM((4, 4, 16, ROUTED), BF),
+            pltpu.VMEM((4, 4, 16, ROUTED), BF),
+            pltpu.VMEM((4, 16, ROUTED), BF),
+            pltpu.VMEM((4, 16, ROUTED), BF),
             dma((4,)),
-            dma((2, 14)), dma((2, SRC, 2)),
+            dma((6, 14)), dma((6, SRC, 2)),
             dma((SRC,)), dma((SRC,)),
             dma((SRC,)), dma((SRC,)),
-            dma((SRC,)), dma((SRC,)),
+            dma((2, SRC)), dma((2, SRC)),
             dma((DEP, 2, 6)), dma((DEP, 2, 6)),
             dma((DEP, 2, 6)), dma((DEP, 2, 6)),
             dma((SRC,)), dma((SRC,)),
-            dma((NDP,)), dma((NDP,)),
-            dma((NDP,)), dma((NDP,)),
-            dma((SRC,)), dma((SRC,)),
+            dma((4, 4)), dma((4, 4)),
+            dma((SRC, SRC)), dma((SRC,)),
         ],
         compiler_params=pltpu.CompilerParams(
             collective_id=0, has_side_effects=True, vmem_limit_bytes=67043328

time: 167 us -> 161 us (0.964)
  Pallas kernels: 166 us -> 160 us
    pallas_call x1, Pallas kernels: 163 us -> 157 us  [per_device(): pl.pallas_call(kernel, out_shape=(jax.ShapeDtypeStruct((TOK, D), BF), jax...]
where the time goes in v3:
time: 161 us
  Pallas kernels  160 us (99%)
    pallas_call x1, Pallas kernels, per_device(): pl.pallas_call(kernel, out_shape=(jax.ShapeDtypeStruct((TOK, D), BF), jax...  157 us
    pallas_call x1, Pallas kernels, per_device(): pl.pallas_call(write_out, out_shape=shapes, in_specs=[vmem] * 4, out_spec...  3.26 us

profile of v3, /device:TPU:0, one launch (start us, length us, event | category | flops | bytes accessed | tf_op | source)
XLA Modules:
  0.0 160.9 jit_solution(5156938228184098702)
XLA Ops:
  0.6 157.0 %moe_backward.1 = (bf16[128,2048]{1,0:T(8,128)(2,1)}, f32[8,4,4,16,128]{4,3,2,1,0:T(8,128)}, bf16[128,3072]{1,0:T(8,128)(2,1)}, bf16[96,2048]{1,0:T(8,128)(2,1)}) custom-call(bf16[128,2048]{1,0:T(8,128)(2,1)} %tokens_hbm.1, bf16[128,2048]{1,0:T(8,128)(2,1)} %grad_hbm.1, f32[1,128]{1,0:T(1,128)} %bitcast.10, bf16[2048,128]{1,0:T(8,128)(2,1)} %rw_ref.1, ...), custom_call_target="tpu_custom_call" | custom-call | tf_op jit(solution)/shard_map/moe_backward/pallas_call | solution.py:703
  157.7 3.3 %write_out.1 = (bf16[128,2048]{1,0:T(8,128)(2,1)}, f32[8,4,4,16,128]{4,3,2,1,0:T(8,128)}, bf16[128,3072]{1,0:T(8,128)(2,1)}, bf16[96,2048]{1,0:T(8,128)(2,1)}) custom-call(bf16[128,2048]{1,0:T(8,128)(2,1)} %get-tuple-element.12.refs_0_, f32[8,4,4,16,128]{4,3,2,1,0:T(8,128)} %get-tuple-element.13.refs_1_, bf16[128,3072]{1,0:T(8,128)(2,1)} %get-tuple-element.14.refs_2_, ...), custom_call_target="tpu_custom_call" | custom-call | tf_op jit(solution)/shard_map/write_out/pallas_call | solution.py:763

commit v4 on v3

--- a/solution.py
+++ b/solution.py
@@ -42,11 +42,12 @@
 
 
 def kernel(
-    tokens_hbm, grad_hbm, z_ref, rw_ref, ids_ref, gu_hbm, dn_hbm,
-    tg_out, rt_out, gug_out, dng_out,
+    tokens_hbm, grad_hbm, z_hbm, rw_hbm, ids_hbm, gu_hbm, dn_hbm,
+    tg_hbm, rt_hbm, gug_hbm, dng_hbm,
+    z_ref, rw_ref, ids_ref, tg_out, rt_out, gug_out, dng_out,
     xa, oa, meta, prob, logit, xr, xt, dy, hid, hidt, pg, gu, dn,
     part, r1, r2, rg, rb, sel, psum, psend, precv, lgrad, rpart, rin, rsum, rbufz, rsumx, rbufx,
-    lsem, ag_s, ag_r, mt_s, mt_r, ps_s, ps_r, rt_s, rt_r, s1, q1, s2, q2, ra_s, ra_r, rs_s, rs_r, rd_s, rd_r,
+    lsem, osem, ag_s, ag_r, mt_s, mt_r, ps_s, ps_r, rt_s, rt_r, s1, q1, s2, q2, ra_s, ra_r, rs_s, rs_r, rd_s, rd_r,
 ):
     dp = lax.axis_index("dp")
     ex = lax.axis_index("expert")
@@ -68,10 +69,10 @@
     cp_grad = pltpu.make_async_copy(grad_hbm, oa.at[0], lsem.at[1])
     cp_gu = pltpu.make_async_copy(gu_hbm, gu, lsem.at[2])
     cp_dn = pltpu.make_async_copy(dn_hbm, dn, lsem.at[3])
+    cp_rw = pltpu.make_async_copy(rw_hbm, rw_ref, lsem.at[4])
+    cp_z = pltpu.make_async_copy(z_hbm, z_ref, lsem.at[5])
+    cp_ids = pltpu.make_async_copy(ids_hbm, ids_ref, lsem.at[6])
     cp_tok.start()
-    cp_grad.start()
-    cp_gu.start()
-    cp_dn.start()
 
     barrier = pltpu.get_barrier_semaphore()
     for k in range(1, 4):
@@ -79,6 +80,12 @@
         pl.semaphore_signal(barrier, inc=1, device_id=(zs(k), ex), device_id_type=MESH)
     for q in range(1, SRC):
         pl.semaphore_signal(barrier, inc=1, device_id=(dp, place[q]), device_id_type=MESH)
+    cp_rw.start()
+    cp_ids.start()
+    cp_z.start()
+    cp_grad.start()
+    cp_gu.start()
+    cp_dn.start()
     pl.semaphore_wait(barrier, 6 + SRC - 1)
 
     OWN = ((0, 0, 4, 2), (0, 1, 2, 4), (0, 1, 4, 2), (0, 0, 2, 4), (0, 0, 1, 1), (0, 1, 1, 1))
@@ -140,6 +147,9 @@
 
     sub = lax.broadcasted_iota(jnp.int32, (TOK, TOK), 0)
     lane = lax.broadcasted_iota(jnp.int32, (TOK, TOK), 1)
+    cp_rw.wait()
+    cp_ids.wait()
+    cp_z.wait()
     lg = nn(xa[0], rw_ref[...])
     logit[...] = lg
     ids = ids_ref[...].astype(F32)
@@ -450,6 +460,14 @@
         z_grad = 2.0 * z * log_total * jnp.exp(lgt - log_total)
         lgrad[...] = (z_grad + scores - prob[...] * mean).astype(BF)
 
+    def gate_copy(k):
+        cols = pl.ds(pl.multiple_of(k * 256, 256), 256)
+        return pltpu.make_async_copy(gug_out.at[:, cols], gug_hbm.at[:, cols], osem.at[k])
+
+    def out_copy(k):
+        a, b = ((dng_out, dng_hbm), (tg_out, tg_hbm), (rt_out, rt_hbm))[k]
+        return pltpu.make_async_copy(a, b, osem.at[NG + k])
+
     def token_grad(half):
         for q in range(1, SRC):
             rt_wait(q, half)
@@ -469,6 +487,8 @@
             return 0
 
         lax.fori_loop(half * 4, half * 4 + 4, one, 0)
+        if half == 1:
+            out_copy(1).start()
 
     def ra_copy(q):
         return pltpu.make_async_remote_copy(
@@ -605,6 +625,7 @@
             rsx(k).wait_send()
             rcx(k, c2).wait_send()
             rcz(k, c1).wait_send()
+        out_copy(2).start()
 
     def body(i, _):
         @pl.when(i < ND)
@@ -675,9 +696,14 @@
         def _():
             stage4(c4, ZD, dng_out, 0)
 
+        @pl.when(c4 == ND - 1)
+        def _():
+            out_copy(0).start()
+
         @pl.when(c4 >= ND)
         def _():
             stage4(c4, ZG, gug_out, ND)
+            gate_copy(c4 - ND).start()
 
         both(i - LAG3, stage3, (ZD,), (ZG,))
         both(i - LAG2, stage2, (ZD,), (ZG,))
@@ -685,19 +711,35 @@
         return 0
 
     lax.fori_loop(0, NC + LAG4, body, 0)
+    for k in range(NG):
+        gate_copy(k).wait()
+    for k in range(3):
+        out_copy(k).wait()
 
 
 def write_out(*refs):
-    sem = refs[8]
-    copies = [pltpu.make_async_copy(refs[k], refs[4 + k], sem.at[k]) for k in range(4)]
-    for c in copies:
-        c.start()
-    for c in copies:
-        c.wait()
+    src, dst, held, sems = refs[0:4], refs[4:8], refs[8:12], refs[12]
+    pieces = []
+    for k in range(4):
+        n = src[k].shape[0] // 2
+        for half in range(2):
+            at = pl.ds(half * n, n)
+            pieces.append(
+                (
+                    pltpu.make_async_copy(src[k].at[at], held[k].at[at], sems.at[0, k, half]),
+                    pltpu.make_async_copy(held[k].at[at], dst[k].at[at], sems.at[1, k, half]),
+                )
+            )
+    for load, _ in pieces:
+        load.start()
+    for load, store in pieces:
+        load.wait()
+        store.start()
+    for _, store in pieces:
+        store.wait()
 
 
 def per_device(tokens, out_grad, z_weight, router_weight, expert_ids, gate_up_weight, down_weight):
-    vmem = pl.BlockSpec(memory_space=pltpu.VMEM)
     hbm = pl.BlockSpec(memory_space=pl.ANY)
     dma = pltpu.SemaphoreType.DMA
     outs = pl.pallas_call(
@@ -708,9 +750,16 @@
             jax.ShapeDtypeStruct((D // 16, 2 * FF), BF),
             jax.ShapeDtypeStruct((FF // 16, D), BF),
         ),
-        in_specs=[hbm, hbm, vmem, vmem, vmem, hbm, hbm],
-        out_specs=(vmem, vmem, vmem, vmem),
+        in_specs=[hbm] * 7,
+        out_specs=(hbm, hbm, hbm, hbm),
         scratch_shapes=[
+            pltpu.VMEM((1, TOK), F32),
+            pltpu.VMEM((D, ROUTED), BF),
+            pltpu.VMEM((4, TOK), jnp.int32),
+            pltpu.VMEM((TOK, D), BF),
+            pltpu.VMEM((SRC, 4, 4, 16, ROUTED), F32),
+            pltpu.VMEM((D // 16, 2 * FF), BF),
+            pltpu.VMEM((FF // 16, D), BF),
             pltpu.VMEM((SRC, TOK, D), BF),
             pltpu.VMEM((SRC, TOK, D), BF),
             pltpu.VMEM((SRC, 16, TOK), F32),
@@ -740,7 +789,7 @@
             pltpu.VMEM((4, 4, 16, ROUTED), BF),
             pltpu.VMEM((4, 16, ROUTED), BF),
             pltpu.VMEM((4, 16, ROUTED), BF),
-            dma((4,)),
+            dma((7,)), dma((NG + 3,)),
             dma((6, 14)), dma((6, SRC, 2)),
             dma((SRC,)), dma((SRC,)),
             dma((SRC,)), dma((SRC,)),
@@ -763,9 +812,9 @@
     token_grad, router_grad, gate_up_grad, down_grad = pl.pallas_call(
         write_out,
         out_shape=shapes,
-        in_specs=[vmem] * 4,
+        in_specs=[hbm] * 4,
         out_specs=[hbm] * 4,
-        scratch_shapes=[dma((4,))],
+        scratch_shapes=[pltpu.VMEM(o.shape, o.dtype) for o in shapes] + [dma((2, 4, 2))],
         name="write_out",
     )(*outs)
     return token_grad, router_grad.reshape(D, ROUTED), gate_up_grad[None], down_grad[None]

time: 161 us -> 159 us (0.988)
  Pallas kernels: 160 us -> 158 us
    pallas_call x1, Pallas kernels: 157 us -> 155 us  [per_device(): pl.pallas_call(kernel, out_shape=(jax.ShapeDtypeStruct((TOK, D), BF), jax...]
where the time goes in v4:
time: 159 us
  Pallas kernels  158 us (99%)
    pallas_call x1, Pallas kernels, per_device(): pl.pallas_call(kernel, out_shape=(jax.ShapeDtypeStruct((TOK, D), BF), jax...  155 us

profile of v4, /device:TPU:0, one launch (start us, length us, event | category | flops | bytes accessed | tf_op | source)
XLA Modules:
  0.0 158.6 jit_solution(17897291354011537030)
XLA Ops:
  0.6 155.2 %moe_backward.1 = (bf16[128,2048]{1,0:T(8,128)(2,1)}, f32[8,4,4,16,128]{4,3,2,1,0:T(8,128)}, bf16[128,3072]{1,0:T(8,128)(2,1)}, bf16[96,2048]{1,0:T(8,128)(2,1)}) custom-call(bf16[128,2048]{1,0:T(8,128)(2,1)} %tokens_hbm.1, bf16[128,2048]{1,0:T(8,128)(2,1)} %grad_hbm.1, f32[1,128]{1,0:T(1,128)} %bitcast.10, bf16[2048,128]{1,0:T(8,128)(2,1)} %rw_hbm.1, ...), custom_call_target="tpu_custom_call" | custom-call | tf_op jit(solution)/shard_map/moe_backward/pallas_call | solution.py:745
  155.9 2.7 %write_out.1 = (bf16[128,2048]{1,0:T(8,128)(2,1)}, f32[8,4,4,16,128]{4,3,2,1,0:T(8,128)}, bf16[128,3072]{1,0:T(8,128)(2,1)}, bf16[96,2048]{1,0:T(8,128)(2,1)}) custom-call(bf16[128,2048]{1,0:T(8,128)(2,1)} %get-tuple-element.12.refs_0_, f32[8,4,4,16,128]{4,3,2,1,0:T(8,128)} %get-tuple-element.13.refs_1_, bf16[128,3072]{1,0:T(8,128)(2,1)} %get-tuple-element.14.refs_2_, ...), custom_call_target="tpu_custom_call" | custom-call | tf_op jit(solution)/shard_map/write_out/pallas_call | solution.py:812

commit v5 on v4

--- a/solution.py
+++ b/solution.py
@@ -224,10 +224,10 @@
         grad_near(part_no)
         grad_far(part_no)
 
-    def forward(lo, hi):
+    def forward(lo, hi, n):
         def run(f, _):
-            a = pl.ds(pl.multiple_of(f * 256, 256), 256)
-            b = pl.ds(pl.multiple_of(FF + f * 256, 256), 256)
+            a = pl.ds(pl.multiple_of(f * n, n), n)
+            b = pl.ds(pl.multiple_of(FF + f * n, n), n)
             g = nn(xr[lo:hi, :], gu[:, a])
             u = nn(xr[lo:hi, :], gu[:, b])
             s = lax.logistic(g)
@@ -241,7 +241,7 @@
 
         return run
 
-    near, far = forward(0, 6 * CAP), forward(6 * CAP, ROWS)
+    near, far = forward(0, 6 * CAP, 256), forward(6 * CAP, ROWS, 512)
     for q in (1, 3, 5):
         ag_side(0, q)
     for q in range(6):
@@ -255,9 +255,9 @@
     ag_near(1)
     ag_side(0, 7)
     gather_tok(7)
-    lax.fori_loop(0, 3, far, 0)
+    lax.fori_loop(0, 2, far, 0)
     ag_relay(2)
-    lax.fori_loop(3, 6, far, 0)
+    lax.fori_loop(2, 3, far, 0)
     ag_near(2)
     grad_part(1)
     cp_dn.wait()

time: 159 us -> 158 us (level)
  no operation moved by 1% of the time
where the time goes in v5:
time: 158 us
  Pallas kernels  157 us (99%)
    pallas_call x1, Pallas kernels, per_device(): pl.pallas_call(kernel, out_shape=(jax.ShapeDtypeStruct((TOK, D), BF), jax...  154 us

profile of v5, /device:TPU:0, one launch (start us, length us, event | category | flops | bytes accessed | tf_op | source)
XLA Modules:
  0.0 157.7 jit_solution(15070624103621404980)
XLA Ops:
  0.6 154.4 %moe_backward.1 = (bf16[128,2048]{1,0:T(8,128)(2,1)}, f32[8,4,4,16,128]{4,3,2,1,0:T(8,128)}, bf16[128,3072]{1,0:T(8,128)(2,1)}, bf16[96,2048]{1,0:T(8,128)(2,1)}) custom-call(bf16[128,2048]{1,0:T(8,128)(2,1)} %tokens_hbm.1, bf16[128,2048]{1,0:T(8,128)(2,1)} %grad_hbm.1, f32[1,128]{1,0:T(1,128)} %bitcast.10, bf16[2048,128]{1,0:T(8,128)(2,1)} %rw_hbm.1, ...), custom_call_target="tpu_custom_call" | custom-call | tf_op jit(solution)/shard_map/moe_backward/pallas_call | solution.py:745
  155.0 2.7 %write_out.1 = (bf16[128,2048]{1,0:T(8,128)(2,1)}, f32[8,4,4,16,128]{4,3,2,1,0:T(8,128)}, bf16[128,3072]{1,0:T(8,128)(2,1)}, bf16[96,2048]{1,0:T(8,128)(2,1)}) custom-call(bf16[128,2048]{1,0:T(8,128)(2,1)} %get-tuple-element.12.refs_0_, f32[8,4,4,16,128]{4,3,2,1,0:T(8,128)} %get-tuple-element.13.refs_1_, bf16[128,3072]{1,0:T(8,128)(2,1)} %get-tuple-element.14.refs_2_, ...), custom_call_target="tpu_custom_call" | custom-call | tf_op jit(solution)/shard_map/write_out/pallas_call | solution.py:812
